TPU v7x, 32 devices: a whole 2x2x4 slice. The times are simulated.
32 devices in a mesh: pair: 2 (over x), tp: 4 (over z), side: 4 (over y, core).
Axes of the slice: x: 2, y: 2, z: 4, core: 2. Of those that a mesh axis runs over, the one named last changes fastest.
Arguments:
- x_prompt: bfloat16 [8, 512, 7168], P(('pair', 'side')), parts along dimension 0
- s_len: int32 [8], P(('pair', 'side')), parts along dimension 0
- y_tok: bfloat16 [8, 4, 7168], P(('pair', 'side')), parts along dimension 0
- k_cache: bfloat16 [8, 1, 4, 64, 128, 192], P(('pair', 'side'), None, None, None, 'tp'), parts along dimension 0
- v_cache: bfloat16 [8, 1, 4, 64, 128, 128], P(('pair', 'side'), None, None, None, 'tp'), parts along dimension 0
- c_len: int32 [8, 4], P(('pair', 'side')), parts along dimension 0
- attn_gain: bfloat16 [1, 7168], replicated
- w_q: bfloat16 [1, 7168, 128, 192], P(None, None, 'tp')
- w_dkv: bfloat16 [1, 7168, 576], replicated
- w_uk: bfloat16 [1, 512, 128, 128], P(None, None, 'tp')
- w_uv: bfloat16 [1, 512, 128, 128], P(None, None, 'tp')
- w_o: bfloat16 [1, 128, 128, 7168], P(None, 'tp')
- mlp_gain: bfloat16 [1, 7168], replicated
- w_gate: bfloat16 [1, 7168, 2048], P(None, None, 'tp')
- w_up: bfloat16 [1, 7168, 2048], P(None, None, 'tp')
- w_down: bfloat16 [1, 2048, 7168], P(None, 'tp')
Outputs:
- output 1: bfloat16 [8, 512, 7168], P(('pair', 'side')), parts along dimension 0
- output 2: bfloat16 [8, 4, 7168], P(('pair', 'side')), parts along dimension 0
- output 3: bfloat16 [8, 1, 512, 128, 192], P(('pair', 'side'), None, None, 'tp'), parts along dimension 0
- output 4: bfloat16 [8, 1, 512, 128, 128], P(('pair', 'side'), None, None, 'tp'), parts along dimension 0
- output 5: bfloat16 [8, 1, 4, 64, 128, 192], P(('pair', 'side'), None, None, None, 'tp'), parts along dimension 0
- output 6: bfloat16 [8, 1, 4, 64, 128, 128], P(('pair', 'side'), None, None, None, 'tp'), parts along dimension 0
There are 2 independent parts. A program takes and returns all parts, laid end to end along the dimension named above; an argument that names none is the same for every part.
All inputs are finite; a program needn't handle non-finite values.
Results may differ from a plain program's by a relative error of at most 0.0109002.
Values are sent between devices in bfloat16 or wider.
A program may use at most 1 GiB of HBM per device.

v0:
```python
import functools
import jax
import jax.numpy as jnp
from jax import lax
from jax.experimental import pallas as pl
from jax.experimental.pallas import tpu as pltpu
from jax.sharding import PartitionSpec as P

EPSILON = 1e-6
THETA = 10000.0
TOK_PAD = 8
dma = pltpu.SemaphoreType.DMA
mesh_id = pl.DeviceIdType.MESH
none = None
END_LAG = 6
RELAY_AT = (12, 21)
MID_LAG = 2


def rms_scaled(values, gain):
    hidden = values.astype(jnp.float32)
    inv_rms = lax.rsqrt(jnp.mean(hidden * hidden, axis=-1, keepdims=True) + EPSILON)
    return (hidden * inv_rms * gain.astype(jnp.float32)).astype(jnp.bfloat16)


def rms_plain(values):
    hidden = values.astype(jnp.float32)
    inv_rms = lax.rsqrt(jnp.mean(hidden * hidden, axis=-1, keepdims=True) + EPSILON)
    return (hidden * inv_rms).astype(jnp.bfloat16)


def apply_rope(values, positions):
    half_dim = values.shape[-1] // 2
    inv_freq = THETA ** (-jnp.arange(half_dim, dtype=jnp.float32) * 2.0 / values.shape[-1])
    angles = positions.astype(jnp.float32)[..., None] * inv_freq
    cos_part = jnp.cos(angles)
    sin_part = jnp.sin(angles)
    first_half = values[..., :half_dim].astype(jnp.float32)
    second_half = values[..., half_dim:].astype(jnp.float32)
    return jnp.concatenate([first_half * cos_part - second_half * sin_part, second_half * cos_part + first_half * sin_part], axis=-1).astype(jnp.bfloat16)


def rope_tables(positions, rope_dim):
    half_dim = rope_dim // 2
    inv_freq = THETA ** (-jnp.arange(half_dim, dtype=jnp.float32) * 2.0 / rope_dim)
    angles = positions.astype(jnp.float32)[..., None] * inv_freq
    return jnp.tile(jnp.cos(angles), (1, 4)), jnp.tile(jnp.sin(angles), (1, 4))


def make_latent(normed, w_dkv_layer, positions, rank_dim):
    latent_raw = jnp.dot(normed, w_dkv_layer, preferred_element_type=jnp.float32).astype(jnp.bfloat16)
    return jnp.concatenate([rms_plain(latent_raw[:, :rank_dim]), apply_rope(latent_raw[:, rank_dim:], positions)], axis=-1)


def expand_latent(latent_pack, w_uk_layer, w_uv_layer):
    rank_dim = w_uk_layer.shape[0]
    latent = latent_pack[:, :rank_dim]
    rope_key = latent_pack[:, rank_dim:]
    key_nope = jnp.einsum('sr,rhn->shn', latent, w_uk_layer, preferred_element_type=jnp.float32).astype(jnp.bfloat16)
    value_full = jnp.einsum('sr,rhv->shv', latent, w_uv_layer, preferred_element_type=jnp.float32).astype(jnp.bfloat16)
    rope_heads = jnp.broadcast_to(rope_key[:, None, :], (key_nope.shape[0], key_nope.shape[1], rope_key.shape[1]))
    return jnp.concatenate([key_nope, rope_heads], axis=-1), value_full


def masked_softmax(scores, allowed):
    return jax.nn.softmax(jnp.where(allowed, scores, -1e30), axis=-1).astype(jnp.bfloat16)


def cache_attention(query_all, key_layer, value_layer, cur_len):
    scores = jnp.einsum('bhe,bthe->bht', query_all, key_layer, preferred_element_type=jnp.float32) * query_all.shape[-1] ** -0.5
    allowed = jnp.arange(key_layer.shape[1])[None, None, :] <= cur_len[:, None, None]
    probs_bf = masked_softmax(scores, allowed)
    return jnp.einsum('bht,bthv->bhv', probs_bf, value_layer, preferred_element_type=jnp.float32).astype(jnp.bfloat16)


def line_barrier(zi, zn, also):
    sem = pltpu.get_barrier_semaphore()

    for one in also:
        pl.semaphore_signal(sem, inc=1, device_id=one, device_id_type=mesh_id)

    @pl.when(zi > 0)
    def _():
        pl.semaphore_signal(sem, inc=1, device_id={'tp': zi - 1}, device_id_type=mesh_id)

    @pl.when(zi < zn - 1)
    def _():
        pl.semaphore_signal(sem, inc=1, device_id={'tp': zi + 1}, device_id_type=mesh_id)

    @pl.when((zi == 0) | (zi == zn - 1))
    def _():
        pl.semaphore_wait(sem, 1 + len(also))

    @pl.when((zi > 0) & (zi < zn - 1))
    def _():
        pl.semaphore_wait(sem, 2 + len(also))


def attend_body(rows, nope, rope, scale, n_ref, w_ref, k_ref, r_ref, v_ref, cos_ref, sin_ref, len_ref, o_ref, qt_ref, acc):
    heads = w_ref.shape[0]
    depth = n_ref.shape[1]
    chunk = depth // 4
    lane = lax.broadcasted_iota(jnp.int32, (1, 2 * rope), 1)
    low = lane < rope
    first = lax.rem(lane, rope) < rope // 2
    wide = heads * (nope + rope)

    def part(c):
        span = pl.ds(pl.multiple_of(c * chunk, 128), chunk)
        return lax.dot_general(n_ref[:, span], w_ref[:, :, span].reshape(wide, chunk), (((1,), (1,)), ((), ())), preferred_element_type=jnp.float32)

    acc[...] = part(0)

    @pl.loop(1, 4)
    def _(c):
        acc[...] = acc[...] + part(c)

    cos, sin = cos_ref[...], sin_ref[...]
    valid = len_ref[0]
    kr = r_ref[...]
    half_rows = rows // 2
    for pair in range(heads // 2):
        base = pair * 2 * (nope + rope)
        t0, t1, t2 = (acc[:, base + nope * i:base + nope * (i + 1)].astype(jnp.bfloat16).astype(jnp.float32) for i in range(3))
        n1 = jnp.where(low, pltpu.roll(t1, rope, 1), pltpu.roll(t2, rope, 1))
        both = jnp.where(low, t1, t2)
        turned = jnp.where(first, -pltpu.roll(both, 2 * rope - rope // 2, 1), pltpu.roll(both, rope // 2, 1))
        both = both * cos + turned * sin
        for sub, nq in ((0, t0), (1, n1)):
            h = pair * 2 + sub
            keep = low if sub == 0 else jnp.logical_not(low)
            query = jnp.concatenate([nq.astype(jnp.bfloat16), jnp.where(keep, both, 0.0).astype(jnp.bfloat16)], axis=1)
            qt_ref[h] = query[rows:]
            for blk in range(2):
                span = (blk + 1) * half_rows
                key = jnp.concatenate([k_ref[h, :, :span], kr[:, :span]], axis=0)
                s = jnp.dot(query[blk * half_rows:(blk + 1) * half_rows], key, preferred_element_type=jnp.float32) * scale
                row = lax.broadcasted_iota(jnp.int32, s.shape, 0) + blk * half_rows
                col = lax.broadcasted_iota(jnp.int32, s.shape, 1)
                s = jnp.where((col <= row) & (col < valid), s, -1e30)
                p = jnp.exp(s - jnp.max(s, axis=1, keepdims=True))
                p = (p * (1.0 / jnp.sum(p, axis=1, keepdims=True))).astype(jnp.bfloat16)
                out = jnp.dot(p, v_ref[h, :span, :], preferred_element_type=jnp.float32)
                o_ref[blk * half_rows:(blk + 1) * half_rows, h * nope:(h + 1) * nope] = out.astype(jnp.bfloat16)


def attend_call(normed, w_q, key_t, rope_t, value, cos, sin, valid_len, rows, scale):
    total, depth = normed.shape
    heads, feat, _ = w_q.shape
    nope = key_t.shape[1]
    rope = feat - nope
    vdim = value.shape[2]
    grp = 4
    vm = pl.BlockSpec(memory_space=pltpu.VMEM)
    return pl.pallas_call(
        functools.partial(attend_body, rows, nope, rope, scale),
        grid=(heads // grp,),
        out_shape=(jax.ShapeDtypeStruct((rows, heads * vdim), jnp.bfloat16), jax.ShapeDtypeStruct((heads, total - rows, 2 * nope), jnp.bfloat16)),
        in_specs=[
            vm,
            pl.BlockSpec((grp, feat, depth), lambda g: (g, 0, 0)),
            pl.BlockSpec((grp, nope, key_t.shape[2]), lambda g: (g, 0, 0)),
            vm,
            pl.BlockSpec((grp, value.shape[1], vdim), lambda g: (g, 0, 0)),
            vm, vm,
            pl.BlockSpec(memory_space=pltpu.SMEM),
        ],
        out_specs=(pl.BlockSpec((rows, grp * vdim), lambda g: (0, g)), pl.BlockSpec((grp, total - rows, 2 * nope), lambda g: (g, 0, 0))),
        scratch_shapes=[pltpu.VMEM((total, grp * feat), jnp.float32)],
        compiler_params=pltpu.CompilerParams(vmem_limit_bytes=60_000_000),
        cost_estimate=pl.CostEstimate(flops=2 * total * depth * heads * feat + 3 * rows * rows * heads * feat, bytes_accessed=heads * feat * depth * 2, transcendentals=rows * rows * heads),
        name='attend',
    )(normed, w_q, key_t, rope_t, value, cos, sin, valid_len)


def reduce_body(zn, nt, tn, hr, p_ref, q_ref, x_ref, t_ref, w_ref, m2_ref, m3_ref, o_ref, ot_ref, g_ref, a_ref, asem, gs, gr, wbuf, pdn, pup, rdn, rup, wsem, sdn, sup, vdn, vup):
    zi = lax.axis_index('tp')

    def wcopy(j):
        return pltpu.make_async_copy(w_ref.at[:, pl.ds(pl.multiple_of(j * tn, 128), tn)], wbuf.at[lax.rem(j, 2)], wsem.at[lax.rem(j, 2)])

    def send_dn(i):
        return pltpu.make_async_remote_copy(pdn.at[i], rdn.at[i], sdn.at[i], vdn.at[i], device_id={'tp': zi - 1}, device_id_type=mesh_id)

    def send_up(i):
        return pltpu.make_async_remote_copy(pup.at[i], rup.at[i], sup.at[i], vup.at[i], device_id={'tp': zi + 1}, device_id_type=mesh_id)

    ends = (zi == 0) | (zi == zn - 1)
    lag = jnp.where(ends, END_LAG, MID_LAG)
    over_y = {'side': lax.rem(lax.axis_index('side') + 2, 4)}
    over_x = {'pair': 1 - lax.axis_index('pair')}
    cut = m2_ref.shape[1] // 2

    def plane(k, c):
        mine = (m2_ref, m3_ref)[k]
        if c < 2:
            src, dst = mine, g_ref.at[k, c]
        elif c == 2:
            src, dst = g_ref.at[k, 0, :, pl.ds(0, cut)], g_ref.at[k, 2, :, pl.ds(0, cut)]
        else:
            src, dst = g_ref.at[k, 1, :, pl.ds(cut, cut)], g_ref.at[k, 2, :, pl.ds(cut, cut)]
        return pltpu.make_async_remote_copy(src, dst, gs.at[k, c], gr.at[k, c], device_id=(over_y, over_x, over_x, over_y)[c], device_id_type=mesh_id)

    wcopy(0).start()
    fill = [
        pltpu.make_async_copy(p_ref, a_ref.at[pl.ds(0, 2 * hr)], asem.at[0]),
        pltpu.make_async_copy(q_ref, a_ref.at[pl.ds(2 * hr, q_ref.shape[0])], asem.at[1]),
    ]
    for one in fill:
        one.start()
    line_barrier(zi, zn, (over_y, over_x))

    @pl.when(ends)
    def _():
        for k in range(2):
            for c in range(2):
                plane(k, c).start()

    for one in fill:
        one.wait()

    def take_dn(i):
        @pl.when(zi < zn - 1)
        def _():
            send_dn(i).wait_recv()
            pdn[i] = pdn[i] + rdn[i]

            @pl.when(zi > 0)
            def _():
                send_dn(i).start()

        @pl.when(zi == 0)
        def _():
            cols = pl.ds(pl.multiple_of(i * tn, 128), tn)
            total = pdn[i]
            o_ref[:, cols] = x_ref[:, cols] + total[:hr].astype(jnp.bfloat16)
            ot_ref[:, cols] = (t_ref[:, cols].astype(jnp.bfloat16) + total[hr:].astype(jnp.bfloat16)).astype(jnp.float32)

    def take_up(i):
        @pl.when(zi > 0)
        def _():
            send_up(i).wait_recv()
            pup[i] = pup[i] + rup[i]

            @pl.when(zi < zn - 1)
            def _():
                send_up(i).start()

            cols = pl.ds(pl.multiple_of(i * tn, 128), tn)
            o_ref[:, cols] = x_ref[:, cols] + pup[i].astype(jnp.bfloat16)
            ot_ref[:, cols] = t_ref[:, cols]

    def handle(i):
        def ordered(near, far):
            @pl.when(i < nt)
            def _():
                near(i)

            @pl.when(i > 0)
            def _():
                far(i - 1)

        @pl.when(zi < zn // 2)
        def _():
            ordered(take_up, take_dn)

        @pl.when(zi >= zn // 2)
        def _():
            ordered(take_dn, take_up)

    @pl.loop(0, nt)
    def _(j):
        wcopy(j).wait()

        @pl.when(j + 1 < nt)
        def _():
            wcopy(j + 1).start()

        wt = wbuf[lax.rem(j, 2)]
        part = jnp.dot(a_ref[...], wt, preferred_element_type=jnp.float32)
        pdn[j, :hr] = part[:hr]
        pdn[j, hr:] = part[2 * hr:2 * hr + TOK_PAD]
        pup[j] = part[hr:2 * hr]

        @pl.when(zi == zn - 1)
        def _():
            send_dn(j).start()

        @pl.when(zi == 0)
        def _():
            send_up(j).start()

        @pl.when(j >= lag)
        def _():
            handle(j - lag)

        for k in range(2):
            @pl.when(ends & (j == RELAY_AT[k]))
            def _(k=k):
                plane(k, 0).wait_recv()
                plane(k, 1).wait_recv()
                plane(k, 2).start()
                plane(k, 3).start()

    @pl.loop(nt - lag, nt + 1)
    def _(j):
        handle(j)

    @pl.loop(0, nt)
    def _(j):
        @pl.when(zi > 0)
        def _():
            send_dn(j).wait_send()

        @pl.when(zi < zn - 1)
        def _():
            send_up(j).wait_send()

    @pl.when(ends)
    def _():
        for k in range(2):
            plane(k, 2).wait_recv()
            plane(k, 3).wait_recv()
            for c in range(4):
                plane(k, c).wait_send()


def reduce_call(p_rows, q_rows, x_own, t_own, w_o, m2, m3, zn):
    hr, width = x_own.shape
    depth = p_rows.shape[1]
    total = p_rows.shape[0] + q_rows.shape[0]
    tn = 256
    nt = width // tn
    td = hr + TOK_PAD
    vm = pl.BlockSpec(memory_space=pltpu.VMEM)
    hb = pl.BlockSpec(memory_space=pl.ANY)
    return pl.pallas_call(
        functools.partial(reduce_body, zn, nt, tn, hr),
        out_shape=(
            jax.ShapeDtypeStruct((hr, width), jnp.bfloat16),
            jax.ShapeDtypeStruct((TOK_PAD, width), jnp.float32),
            jax.ShapeDtypeStruct((2, 3) + m2.shape, jnp.bfloat16),
        ),
        in_specs=[hb, hb, vm, vm, hb, hb, hb],
        out_specs=(vm, vm, hb),
        scratch_shapes=[
            pltpu.VMEM((total, depth), jnp.bfloat16),
            dma((2,)),
            dma((2, 4)),
            dma((2, 4)),
            pltpu.VMEM((2, depth, tn), jnp.bfloat16),
            pltpu.VMEM((nt, td, tn), jnp.float32),
            pltpu.VMEM((nt, hr, tn), jnp.float32),
            pltpu.VMEM((nt, td, tn), jnp.float32),
            pltpu.VMEM((nt, hr, tn), jnp.float32),
            dma((2,)),
            dma((nt,)),
            dma((nt,)),
            dma((nt,)),
            dma((nt,)),
        ],
        compiler_params=pltpu.CompilerParams(collective_id=0, has_side_effects=True, vmem_limit_bytes=66_000_000),
        cost_estimate=pl.CostEstimate(flops=2 * total * depth * width, bytes_accessed=depth * width * 2, transcendentals=0),
        name='wo_reduce',
    )(p_rows, q_rows, x_own, t_own, w_o, m2, m3)


def mlp_body(zn, nq, hr, cw, *refs):
    b_ref, h_ref, t_ref, wg_ref, wu_ref, wd_ref = refs[:6]
    half = nq // 2
    n_in = nq + 3
    pieces = refs[6:6 + nq]
    plane_own, spread = refs[6 + nq:8 + nq], refs[8 + nq]
    o_ref, ot_ref, xc_ref, gacc, uacc, m_ref, wbuf, obuf, dbuf, wsem, dsem, xs, xr, sa, ra, sb, rb, st, rt = refs[6 + n_in:]
    zi = lax.axis_index('tp')
    side = lax.axis_index('side')
    qi = lax.axis_index('pair') * (nq // 2) + side
    slots = 4
    steps = slots * nq
    depth = 4

    def flip(e):
        out = 0
        for bit in (1, 2, 4):
            out = out + bit * lax.rem(lax.rem(qi // bit, 2) + lax.rem(e // bit, 2), 2)
        return out

    def cols_at(q):
        return pl.ds(pl.multiple_of(q * cw, 128), cw)

    order = [(s, e) for s in (0, 1) for e in range(nq)]
    order += [(s, e) for par in (0, 1) for s in (2, 3) for e in range(par, nq, 2)]

    def slot_piece(i):
        late = i - 2 * nq
        early = i < 2 * nq
        s = jnp.where(early, i // nq, 2 + lax.rem(late // half, 2))
        e = jnp.where(early, lax.rem(i, nq), 2 * lax.rem(late, half) + late // (2 * half))
        return s, e

    partner = {'side': side + 1 - 2 * lax.rem(side, 2)}

    def at_hand(k, j):
        return plane_own[k] if j == 0 else spread.at[k, j - 1]

    def cross(k, j):
        return pltpu.make_async_remote_copy(at_hand(k, j), xc_ref.at[k, j], xs.at[k, j], xr.at[k, j], device_id=partner, device_id_type=mesh_id)

    def source(s, e):
        if s == 1:
            return pieces[e]
        if e % 2 == 0:
            return at_hand(s - 2, e // 2)
        return xc_ref.at[s - 2, e // 2]

    line_barrier(zi, zn, (partner,))
    ends = (zi == 0) | (zi == zn - 1)

    def start_gu(i):
        buf = lax.rem(i, depth)

        @pl.when(i < nq)
        def _():
            rows = cols_at(flip(i))
            pltpu.make_async_copy(wg_ref.at[rows, :], wbuf.at[buf, 0], wsem.at[buf]).start()
            pltpu.make_async_copy(wu_ref.at[rows, :], wbuf.at[buf, 1], wsem.at[buf]).start()

        for k, (s, e) in enumerate(order):
            if s > 0:
                @pl.when(i == k)
                def _(s=s, e=e):
                    if s > 1 and e % 2:
                        cross(s - 2, e // 2).wait_recv()
                    pltpu.make_async_copy(source(s, e).at[pl.ds(0, 2)], wbuf.at[buf], wsem.at[buf]).start()

    def start_dn(e):
        pltpu.make_async_copy(wd_ref.at[:, cols_at(flip(e))], obuf.at[lax.rem(e, 2)], dsem.at[lax.rem(e, 2), 0]).start()
        for k in range(nq):
            @pl.when(e == k)
            def _(k=k):
                for s in range(1, slots):
                    pltpu.make_async_copy(source(s, k).at[2], dbuf.at[lax.rem(e, 2), s - 1], dsem.at[lax.rem(e, 2), s]).start()

    hh = hr // 2

    def block(h, r, q):
        return o_ref.at[pl.ds(h * hr + r * hh, hh), cols_at(q)]

    def up(q, r):
        return pltpu.make_async_remote_copy(block(0, r, q), block(0, r, q), sa.at[r, q], ra.at[r, q], device_id={'tp': zi + 1}, device_id_type=mesh_id)

    def down(q, r):
        return pltpu.make_async_remote_copy(block(1, r, q), block(1, r, q), sb.at[r, q], rb.at[r, q], device_id={'tp': zi - 1}, device_id_type=mesh_id)

    def tok(q):
        tile = ot_ref.at[:, cols_at(q)]
        return pltpu.make_async_remote_copy(tile, tile, st.at[q], rt.at[q], device_id={'tp': zi + 1}, device_id_type=mesh_id)

    @pl.when(ends)
    def _():
        for k in range(2):
            for j in range(half):
                cross(k, j).start()
        for i in range(depth - 1):
            start_gu(jnp.int32(i))
        gacc[...] = jnp.zeros_like(gacc)
        uacc[...] = jnp.zeros_like(uacc)

        @pl.loop(0, steps)
        def _(i):
            buf = lax.rem(i, depth)
            s, e = slot_piece(i)
            pltpu.make_async_copy(pieces[0].at[pl.ds(0, 2)], wbuf.at[buf], wsem.at[buf]).wait()

            @pl.when(i + depth - 1 < steps)
            def _():
                start_gu(i + depth - 1)

            rows = b_ref[:, cols_at(flip(e))]
            gacc[s] = gacc[s] + jnp.dot(rows, wbuf[buf, 0], preferred_element_type=jnp.float32)
            uacc[s] = uacc[s] + jnp.dot(rows, wbuf[buf, 1], preferred_element_type=jnp.float32)

        start_dn(jnp.int32(0))

        @pl.loop(0, slots)
        def _(s):
            gate = gacc[s]
            m_ref[s] = (gate * jax.nn.sigmoid(gate) * uacc[s]).astype(jnp.bfloat16)

        @pl.loop(0, nq)
        def _(e):
            par = lax.rem(e, 2)
            q = flip(e)
            cols = cols_at(q)

            @pl.when(e + 1 < nq)
            def _():
                start_dn(e + 1)

            acc = None
            for s in range(slots):
                pltpu.make_async_copy(pieces[0].at[2], dbuf.at[par, max(s - 1, 0)], dsem.at[par, s]).wait()
                if s == 0:
                    acc = jnp.dot(m_ref[s], obuf[par], preferred_element_type=jnp.float32)
                else:
                    acc = acc + lax.dot_general(m_ref[s], dbuf[par, s - 1], (((1,), (1,)), ((), ())), preferred_element_type=jnp.float32)
            res = h_ref[:, cols] + acc[:hr].astype(jnp.bfloat16)

            @pl.when(zi == 0)
            def _():
                o_ref[:hr, cols] = res
                ot_ref[:, cols] = (t_ref[:, cols].astype(jnp.bfloat16) + acc[hr:hr + TOK_PAD].astype(jnp.bfloat16)).astype(jnp.float32)
                up(q, 0).start()
                up(q, 1).start()
                tok(q).start()

            @pl.when(zi == zn - 1)
            def _():
                o_ref[hr:, cols] = res
                down(q, 0).start()
                down(q, 1).start()

        for k in range(2):
            for j in range(half):
                cross(k, j).wait_send()

    @pl.when((zi > 0) & (zi < zn - 1))
    def _():
        @pl.loop(0, 2 * nq + 1)
        def _(i):
            def pass_up(n):
                q = flip(n // 2)
                up(q, lax.rem(n, 2)).wait_recv()
                up(q, lax.rem(n, 2)).start()

                @pl.when(lax.rem(n, 2) == 1)
                def _():
                    tok(q).wait_recv()
                    tok(q).start()

            def pass_down(n):
                q = flip(n // 2)
                down(q, lax.rem(n, 2)).wait_recv()
                down(q, lax.rem(n, 2)).start()

            def ordered(near, far):
                @pl.when(i < 2 * nq)
                def _():
                    near(i)

                @pl.when(i > 0)
                def _():
                    far(i - 1)

            @pl.when(zi < zn // 2)
            def _():
                ordered(pass_up, pass_down)

            @pl.when(zi >= zn // 2)
            def _():
                ordered(pass_down, pass_up)

    @pl.loop(0, nq)
    def _(q):
        @pl.when(zi == zn - 1)
        def _():
            up(q, 0).wait_recv()
            up(q, 1).wait_recv()
            tok(q).wait_recv()

        @pl.when(zi == 0)
        def _():
            down(q, 0).wait_recv()
            down(q, 1).wait_recv()

        @pl.when(zi < zn - 1)
        def _():
            up(q, 0).wait_send()
            up(q, 1).wait_send()
            tok(q).wait_send()

        @pl.when(zi > 0)
        def _():
            down(q, 0).wait_send()
            down(q, 1).wait_send()


def mlp_call(b_rows, h_rows, t_rows, w_gate, w_up, w_down, pieces, zn):
    hr, width = h_rows.shape
    br = b_rows.shape[0]
    nq = len(pieces) - 3
    fw = w_gate.shape[1]
    cw = width // nq
    vm = pl.BlockSpec(memory_space=pltpu.VMEM)
    hb = pl.BlockSpec(memory_space=pl.ANY)
    out = pl.pallas_call(
        functools.partial(mlp_body, zn, nq, hr, cw),
        out_shape=(
            jax.ShapeDtypeStruct((2 * hr, width), jnp.bfloat16),
            jax.ShapeDtypeStruct((TOK_PAD, width), jnp.float32),
            jax.ShapeDtypeStruct((2, nq // 2, 3, cw, fw), jnp.bfloat16),
        ),
        in_specs=[vm, vm, vm] + [hb] * (3 + len(pieces)),
        out_specs=(vm, vm, hb),
        scratch_shapes=[
            pltpu.VMEM((4, br, fw), jnp.float32),
            pltpu.VMEM((4, br, fw), jnp.float32),
            pltpu.VMEM((4, br, fw), jnp.bfloat16),
            pltpu.VMEM((4, 2, cw, fw), jnp.bfloat16),
            pltpu.VMEM((2, fw, cw), jnp.bfloat16),
            pltpu.VMEM((2, 3, cw, fw), jnp.bfloat16),
            dma((4,)),
            dma((2, 4)),
            dma((2, nq // 2)),
            dma((2, nq // 2)),
        ] + [dma((2, nq)) for _ in range(4)] + [dma((nq,)) for _ in range(2)],
        compiler_params=pltpu.CompilerParams(collective_id=1, has_side_effects=True, vmem_limit_bytes=60_000_000),
        cost_estimate=pl.CostEstimate(flops=2 * br * 4 * fw * width * 3, bytes_accessed=4 * fw * width * 6, transcendentals=0),
        name='mlp_spread',
    )(b_rows, h_rows, t_rows, w_gate, w_up, w_down, *pieces)
    return out[0], out[1]


def own_piece(w_gate, w_up, w_down, nq):
    qi = lax.axis_index('pair') * (nq // 2) + lax.axis_index('side')
    cw = w_gate.shape[0] // nq
    return jnp.stack([
        lax.dynamic_slice_in_dim(w_gate, qi * cw, cw, 0),
        lax.dynamic_slice_in_dim(w_up, qi * cw, cw, 0),
        lax.dynamic_slice_in_dim(w_down, qi * cw, cw, 1).T,
    ])


def to_ends(piece, step, zn):
    return lax.ppermute(piece, 'tp', [(step, 0), (zn - 1 - step, zn - 1)])


def plane_step(mine):
    over_y = lax.ppermute(mine, 'side', [(0, 2), (2, 0), (1, 3), (3, 1)])
    over_x = lax.ppermute(mine, 'pair', [(0, 1), (1, 0)])
    over_d = lax.ppermute(mine, ('pair', 'side'), [(p * 4 + s, (1 - p) * 4 + (s + 2) % 4) for p in range(2) for s in range(4)])
    return [mine, over_y, over_x, over_d]


def core_step(parts):
    out = []
    for part in parts:
        out += [part, lax.ppermute(part, 'side', [(0, 1), (1, 0), (2, 3), (3, 2)])]
    return out


def tie(*values):
    return lax.optimization_barrier(values)


def solution(mesh):
    groups = mesh.shape['side']
    zn = mesh.shape['tp']
    nq = mesh.shape['pair'] * groups
    shift_pairs = [(source_idx, (source_idx + 1) % groups) for source_idx in range(groups)]
    group_axes = ('pair', 'side')
    head_spec = P(none, none, 'tp', none)
    cache_spec = P(group_axes, none, none, none, 'tp', none)
    prompt_spec = P(group_axes, none, none, 'tp', none)
    row_spec = P(group_axes, none, none)
    spec_in = (row_spec, P(group_axes), row_spec, cache_spec, cache_spec, P(group_axes, none), P(), head_spec, P(), head_spec, head_spec, P(none, 'tp', none, none), P(), P(none, none, 'tp'), P(none, none, 'tp'), P(none, 'tp', none))
    spec_out = (row_spec, row_spec, prompt_spec, prompt_spec, cache_spec, cache_spec)

    def device_step(x_prompt, s_len, y_tok, k_cache, v_cache, c_len, attn_gain, w_q, w_dkv, w_uk, w_uv, w_o, mlp_gain, w_gate, w_up, w_down):
        layer = (attn_gain, w_q, w_dkv, w_uk, w_uv, w_o, mlp_gain, w_gate, w_up, w_down)
        attn_gain, w_q, w_dkv, w_uk, w_uv, w_o, mlp_gain, w_gate, w_up, w_down = (v[0] for v in layer)
        zi = lax.axis_index('tp')
        hidden, toks = x_prompt[0], y_tok[0]
        rows, width = hidden.shape
        nb = toks.shape[0]
        hr = rows // 2
        cur_len = c_len[0]
        own = own_piece(w_gate, w_up, w_down, nq)
        near = to_ends(own, 1, zn)

        every = jnp.concatenate([hidden, toks, jnp.zeros((16 - nb, width), hidden.dtype)], axis=0)
        positions = jnp.concatenate([jnp.arange(rows, dtype=jnp.int32), cur_len, jnp.zeros((16 - nb,), jnp.int32)])
        normed = rms_scaled(every, attn_gain)
        latent_pack = make_latent(normed, w_dkv, positions, w_uk.shape[0])
        received = lax.ppermute(latent_pack[:rows], 'side', shift_pairs)
        nope, rank = w_uk.shape[-1], w_uk.shape[0]
        heads, rope = w_q.shape[1], w_q.shape[2] - nope
        latent, rope_key = latent_pack[:, :rank], latent_pack[:, rank:]
        key_t = jnp.einsum('sr,rhn->hns', latent, w_uk, preferred_element_type=jnp.float32).astype(jnp.bfloat16)
        value = jnp.einsum('sr,rhv->hsv', latent, w_uv, preferred_element_type=jnp.float32).astype(jnp.bfloat16)
        cos, sin = rope_tables(positions, rope)
        rope_t = jnp.concatenate([rope_key[:rows].T] * 2, axis=0)
        normed, own, near = tie(normed, own, near)
        first = plane_step(near)
        middle = to_ends(own, 2, zn)
        far = to_ends(own, 3, zn)
        p_rows, q_tok = attend_call(normed, w_q.transpose(1, 2, 0), key_t, rope_t, value, cos, sin, s_len, rows, w_q.shape[2] ** -0.5)

        q_rope = q_tok[:, :nb, nope:nope + rope] + q_tok[:, :nb, nope + rope:]
        query_tok = jnp.concatenate([q_tok[:, :nb, :nope], q_rope], axis=-1).transpose(1, 0, 2)
        rope_new = jnp.broadcast_to(rope_key[rows:rows + nb, None, :], (nb, heads, rope))
        key_new = jnp.concatenate([key_t[:, :, rows:rows + nb].transpose(2, 0, 1), rope_new], axis=-1)
        value_new = value[:, rows:rows + nb].transpose(1, 0, 2)
        key_old, value_old = k_cache[0, 0], v_cache[0, 0]
        slot_hit = (jnp.arange(key_old.shape[1])[None, :] == cur_len[:, None])[:, :, None, None]
        key_layer = jnp.where(slot_hit, key_new[:, None], key_old)
        value_layer = jnp.where(slot_hit, value_new[:, None], value_old)
        tok_val = cache_attention(query_tok, key_layer, value_layer, cur_len).reshape(nb, -1)
        q_rows = jnp.concatenate([tok_val, jnp.zeros((16 - nb, tok_val.shape[1]), tok_val.dtype)], axis=0)

        p_rows, received = tie(p_rows, received)
        x_own = lax.dynamic_slice_in_dim(hidden, jnp.where(zi < zn // 2, 0, hr), hr, 0)
        t_own = jnp.concatenate([toks, jnp.zeros((TOK_PAD - nb, width), toks.dtype)], axis=0).astype(jnp.float32)
        h_mid, t_mid, spread = reduce_call(p_rows, q_rows, x_own, t_own, w_o.reshape(-1, width), middle, far, zn)
        h_mid, first = tie(h_mid, first)
        pieces = core_step(first) + [middle, far, spread]

        key_in, value_in = expand_latent(received, w_uk, w_uv)

        b_rows = jnp.concatenate([
            rms_scaled(h_mid, mlp_gain),
            rms_scaled(t_mid.astype(jnp.bfloat16), mlp_gain),
            jnp.zeros((TOK_PAD, width), jnp.bfloat16),
        ], axis=0)
        h_out, t_out = mlp_call(b_rows, h_mid, t_mid, w_gate, w_up, w_down, pieces, zn)
        y_out = t_out[:nb].astype(jnp.bfloat16)
        return (h_out[None], y_out[None], key_in[None, None], value_in[None, None], key_layer[None, None], value_layer[None, None])

    return jax.shard_map(device_step, mesh=mesh, in_specs=spec_in, out_specs=spec_out, check_vma=False)
```

profile of v0, /device:TPU:0, one launch (start us, length us, event | category | flops | bytes accessed | tf_op | source)
XLA Modules:
  0.0 593.9 jit_solution(5890120755084688165)
XLA Ops:
  0.6 1.3 constant_dynamic-slice_fusion
  1.9 0.5 copy.94
  2.5 1.7 constant_dynamic-slice_fusion.1
  4.2 1.8 pad_maximum_fusion
  6.0 1.4 collective-permute-start
  7.6 2.5 fusion.2
  10.2 7.6 %fusion.4.n_ref = bf16[528,7168]{1,0:T(8,128)(2,1)S(1)} fusion(f32[7168]{0:T(1024)S(1)} %bitcast.96, f32[528]{0:T(1024)S(1)} %add_rsqrt_fusion.1, bf16[4,7168]{1,0:T(4,128)(2,1)S(1)} %bitcast.91, bf16[512,7168]{1,0:T(8,128)(2,1)S(1)} %bitcast.78, bf16[528]{0:T(1024)(128)(2,1)S(1)} %pad.26.clone), kind=kLoop, calls=%fused_computation.6 | loop fusion | flops 34062336 | bytes 14998624 | tf_op jit(solution)/shard_map/convert_element_type | solution.py:23
  17.8 6.6 %fusion.22 = bf16[528,576]{0,1:T(8,128)(2,1)S(1)} fusion(bf16[528,7168]{1,0:T(8,128)(2,1)S(1)} %fusion.4.n_ref, bf16[1,7168,576]{1,2,0:T(8,128)(2,1)S(1)} %bitcast.105), kind=kOutput, calls=%fused_computation.36 | convolution fusion | flops 4360283136 | bytes 16435200 | tf_op jit(solution)/shard_map/dot_general | solution.py:51
  24.4 0.2 fusion.25
  24.8 0.4 fusion.46
  25.2 0.9 pad_maximum_fusion.1
  26.1 0.9 collective-permute-start.1
  27.1 2.7 convert_bitcast_fusion.v_ref
  29.9 0.5 bitcast_select_fusion.1
  30.3 2.1 broadcast_select_fusion.1
  32.5 7.5 %copy.108 = bf16[512,32,128]{0,2,1:T(8,128)(2,1)} copy(bf16[512,32,128]{2,1,0:T(8,128)(2,1)} %bitcast.86) | data formatting | bytes 8388608 | tf_op jit(solution)/shard_map/squeeze | solution.py:671
  40.0 5.2 fusion.33
  45.2 3.2 copy.146
  48.3 8.8 %copy.99 = bf16[528,32,128]{0,2,1:T(8,128)(2,1)} copy(bf16[528,32,128]{2,1,0:T(8,128)(2,1)} %copy.146) | data formatting | bytes 8650752 | tf_op jit(solution)/shard_map/convert_element_type | solution.py:689
  57.2 0.9 copy.102.cos_ref
  58.1 0.8 copy.103.sin_ref
  59.6 1.3 slice_bitcast_fusion
  61.0 0.4 copy.105
  61.5 0.7 pad_maximum_fusion.3.r_ref
  62.2 2.6 bitcast_select_fusion
  64.8 0.8 copy-done.1
  65.6 2.4 broadcast_select_fusion
  68.0 0.7 pad_convert_fusion.t_ref
  68.7 0.9 slice-done.1
  69.6 2.1 dynamic-slice_bitcast_fusion.x_ref
  71.7 1.3 collective-permute-start.2
  73.0 6.5 %collective-permute-start.3 = (bf16[3,896,512]{2,1,0:T(8,128)(2,1)}, bf16[3,896,512]{2,1,0:T(8,128)(2,1)}, u32[]{:S(2)}, u32[]{:S(2)}) collective-permute-start(bf16[3,896,512]{2,1,0:T(8,128)(2,1)} %pad_maximum_fusion), channel_id=1, source_target_pairs={{12,0},{0,12},{13,1},{1,13},{14,2},{2,14},{15,3},{3,15},{28,16},{1... | collective-permute-start | bytes 8257544 | tf_op jit(solution)/shard_map/ppermute | solution.py:635
  79.5 1.6 collective-permute-start.4
  81.1 1.5 collective-permute-start.5
  82.6 90.5 %attend.1 = (bf16[512,4096]{1,0:T(8,128)(2,1)}, bf16[32,16,256]{2,1,0:T(8,128)(2,1)}) custom-call(bf16[528,7168]{1,0:T(8,128)(2,1)} %copy-done.4, bf16[32,192,7168]{2,1,0:T(8,128)(2,1)} %bitcast.7.w_ref, bf16[32,128,528]{2,1,0:T(8,128)(2,1)} %bitcast.84, bf16[128,512]{1,0:T(8,128)(2,1)} %pad_maximum_fusion.3.r_ref, bf16[32,528,128]{2,1,0:T(8,128)(2,1)} %copy-done.10, ...), custom_call_target="tpu_custom_call" | custom-call | flops 51338280960 | bytes 88080384 | tf_op jit(solution)/shard_map/attend/pallas_call | solution.py:155
  173.0 0.9 slice.51
  173.9 1.0 slice_add_fusion
  175.0 2.4 fusion.10
  177.3 0.2 fusion.31
  177.6 0.7 fusion.20
  178.3 0.7 concatenate.52.q_ref
  179.0 0.5 collective-permute-start.6
  179.5 0.8 slice.59
  180.3 4.7 fusion.37
  185.0 0.6 convert_element_type.96
  185.7 1.5 copy-done.12
  187.2 3.9 convert_bitcast_fusion.1
  191.2 4.7 copy.112
  195.9 0.2 broadcast_in_dim.115
  196.1 3.1 maximum_bitcast_fusion
  199.2 222.4 %wo_reduce.1 = (bf16[256,7168]{1,0:T(8,128)(2,1)}, f32[8,7168]{1,0:T(8,128)}, bf16[2,3,3,896,512]{4,3,2,1,0:T(8,128)(2,1)}) custom-call(bf16[512,4096]{1,0:T(8,128)(2,1)} %get-tuple-element.25.p_ref, bf16[16,4096]{1,0:T(8,128)(2,1)} %concatenate.52.q_ref, bf16[256,7168]{1,0:T(8,128)(2,1)} %dynamic-slice_bitcast_fusion.x_ref, ...), custom_call_target="tpu_custom_call" | custom-call | flops 31004295168 | bytes 58720256 | tf_op jit(solution)/shard_map/wo_reduce/pallas_call | solution.py:337
  421.7 3.0 fusion.7
  424.7 1.2 fusion.39
  425.9 0.5 collective-permute-start.7
  426.5 0.4 collective-permute-start.9
  427.0 1.1 fusion.9
  428.1 2.9 maximum_maximum_fusion.1.refs_0_
  431.1 0.2 collective-permute-done.10.refs_13_
  431.2 4.1 collective-permute-done.7.refs_7_
  435.3 3.9 collective-permute-done.8.refs_9_
  439.2 3.9 collective-permute-done.9.refs_11_
  443.2 142.3 %mlp_spread.1 = (bf16[512,7168]{1,0:T(8,128)(2,1)}, f32[8,7168]{1,0:T(8,128)}, bf16[2,4,3,896,512]{4,3,2,1,0:T(8,128)(2,1)}) custom-call(bf16[272,7168]{1,0:T(8,128)(2,1)} %maximum_maximum_fusion.1.refs_0_, bf16[256,7168]{1,0:T(8,128)(2,1)} %get-tuple-element.30.refs_1_, f32[8,7168]{1,0:T(8,128)} %get-tuple-element.31.refs_2_, bf16[7168,512]{1,0:T(8,128)(2,1)} %bitcast.99, ...), custom_call_target="tpu_custom_call" | custom-call | flops 23957864448 | bytes 88080384 | tf_op jit(solution)/shard_map/mlp_spread/pallas_call | solution.py:596
  585.5 1.6 fusion.51
  587.1 6.6 %copy.150 = bf16[1,512,7168]{2,1,0:T(8,128)(2,1)} copy(bf16[1,512,7168]{2,1,0:T(8,128)(2,1)} %bitcast.85) | data formatting | bytes 14680064
  (73 shorter events, 1.2 us)
Async XLA Ops:
  2.4 5.1 copy-start
  2.5 5.1 copy-start.6
  6.0 4.1 copy-start.7
  6.0 65.6 %collective-permute-start = (bf16[3,896,512]{2,1,0:T(8,128)(2,1)}, bf16[3,896,512]{2,1,0:T(8,128)(2,1)}, u32[]{:S(2)}, u32[]{:S(2)}) collective-permute-start(bf16[3,896,512]{2,1,0:T(8,128)(2,1)} %pad_maximum_fusion), channel_id=1, source_target_pairs={{4,0},{8,12},{5,1},{9,13},{6,2},{10,14},{7,3},{11,15},{20,16},{24,... | collective-permute-start | bytes 8257544 | tf_op jit(solution)/shard_map/ppermute | solution.py:635
  7.6 10.2 %slice-start.2 = ((s8[8257536]{0:T(1024)(128)(4,1)}), s8[4194304]{0:T(1024)(128)(4,1)S(1)}, s32[]{:S(2)}) async-start(s8[8257536]{0:T(1024)(128)(4,1)} %bitcast.104), calls=%async_computation.2 | async-start | bytes 8388608
  10.2 7.6 %slice-start.3 = ((s8[8257536]{0:T(1024)(128)(4,1)}), s8[4063232]{0:T(1024)(128)(4,1)S(1)}, s32[]{:S(2)}) async-start(s8[8257536]{0:T(1024)(128)(4,1)} %bitcast.104), calls=%async_computation.3 | async-start | bytes 8126464
  17.8 6.6 %copy-start.4 = (bf16[528,7168]{1,0:T(8,128)(2,1)}, bf16[528,7168]{1,0:T(8,128)(2,1)S(1)}, u32[]{:S(2)}) copy-start(bf16[528,7168]{1,0:T(8,128)(2,1)S(1)} %fusion.4.n_ref) | copy-start | bytes 22708228
  17.8 7.0 %copy-start.9 = (s32[1,4]{1,0:T(1,128)S(1)}, s32[1,4]{1,0:T(1,128)}, u32[]{:S(2)}) copy-start(s32[1,4]{1,0:T(1,128)} %param.21) | copy-start | bytes 52
  17.8 9.3 %copy-start.11 = (bf16[1,512,32,128]{3,2,1,0:T(8,128)(2,1)S(1)}, bf16[1,512,32,128]{3,2,1,0:T(8,128)(2,1)}, u32[]{:S(2)}) copy-start(bf16[1,512,32,128]{3,2,1,0:T(8,128)(2,1)} %param.26) | copy-start | bytes 12582916
  26.1 152.9 %collective-permute-start.1 = (bf16[512,576]{0,1:T(8,128)(2,1)}, bf16[512,576]{0,1:T(8,128)(2,1)}, u32[]{:S(2)}, u32[]{:S(2)}) collective-permute-start(bf16[512,576]{0,1:T(8,128)(2,1)} %pad_maximum_fusion.1), channel_id=1, source_target_pairs={{0,1},{1,2},{2,3},{3,0},{4,5},{5,6},{6,7},{7,4},{8,9},{9,10},{10,1... | collective-permute-start | bytes 1769480 | tf_op jit(solution)/shard_map/ppermute | solution.py:685
  27.1 2.7 copy-start.3
  29.8 2.7 copy-start.10
  57.1 4.2 copy-start.8
  62.2 3.4 copy-start.1
  62.2 6.5 %slice-start = ((s8[7340032]{0:T(1024)(128)(4,1)}), s8[4194304]{0:T(1024)(128)(4,1)S(1)}, s32[]{:S(2)}) async-start(s8[7340032]{0:T(1024)(128)(4,1)} %bitcast.79), calls=%async_computation | async-start | bytes 8388608
  65.6 4.0 slice-start.1
  71.7 127.6 %collective-permute-start.2 = (bf16[3,896,512]{2,1,0:T(8,128)(2,1)}, bf16[3,896,512]{2,1,0:T(8,128)(2,1)}, u32[]{:S(2)}, u32[]{:S(2)}) collective-permute-start(bf16[3,896,512]{2,1,0:T(8,128)(2,1)} %pad_maximum_fusion), channel_id=1, source_target_pairs={{8,0},{4,12},{9,1},{5,13},{10,2},{6,14},{11,3},{7,15},{24,16},{20,... | collective-permute-start | bytes 8257544 | tf_op jit(solution)/shard_map/ppermute | solution.py:635
  73.0 126.3 %collective-permute-start.3 = (bf16[3,896,512]{2,1,0:T(8,128)(2,1)}, bf16[3,896,512]{2,1,0:T(8,128)(2,1)}, u32[]{:S(2)}, u32[]{:S(2)}) collective-permute-start(bf16[3,896,512]{2,1,0:T(8,128)(2,1)} %pad_maximum_fusion), channel_id=1, source_target_pairs={{12,0},{0,12},{13,1},{1,13},{14,2},{2,14},{15,3},{3,15},{28,16},{1... | collective-permute-start | bytes 8257544 | tf_op jit(solution)/shard_map/ppermute | solution.py:635
  79.5 342.2 %collective-permute-start.4 = (bf16[3,896,512]{2,1,0:T(8,128)(2,1)}, bf16[3,896,512]{2,1,0:T(8,128)(2,1)}, u32[]{:S(2)}, u32[]{:S(2)}) collective-permute-start(bf16[3,896,512]{2,1,0:T(8,128)(2,1)} %collective-permute-done.refs_6_), channel_id=1, source_target_pairs={{0,2},{2,0},{1,3},{3,1},{4,6},{6,4},{5,7},{7,5},{8,10},{10,8},{9,1... | collective-permute-start | bytes 8257544 | tf_op jit(solution)/shard_map/ppermute | solution.py:639
  81.1 340.6 %collective-permute-start.5 = (bf16[3,896,512]{2,1,0:T(8,128)(2,1)}, bf16[3,896,512]{2,1,0:T(8,128)(2,1)}, u32[]{:S(2)}, u32[]{:S(2)}) collective-permute-start(bf16[3,896,512]{2,1,0:T(8,128)(2,1)} %collective-permute-done.refs_6_), channel_id=1, source_target_pairs={{0,16},{16,0},{1,17},{17,1},{2,18},{18,2},{3,19},{19,3},{4,20},{20... | collective-permute-start | bytes 8257544 | tf_op jit(solution)/shard_map/ppermute | solution.py:640
  179.0 242.7 %collective-permute-start.6 = (bf16[3,896,512]{2,1,0:T(8,128)(2,1)}, bf16[3,896,512]{2,1,0:T(8,128)(2,1)}, u32[]{:S(2)}, u32[]{:S(2)}) collective-permute-start(bf16[3,896,512]{2,1,0:T(8,128)(2,1)} %collective-permute-done.refs_6_), channel_id=1, source_target_pairs={{0,18},{1,19},{2,16},{3,17},{16,2},{17,3},{18,0},{19,1},{4,22},{5,... | collective-permute-start | bytes 8257544 | tf_op jit(solution)/shard_map/ppermute | solution.py:641
  185.0 2.2 copy-start.12
  421.6 5.3 copy-start.2
  424.7 3.3 copy-start.5
  425.9 5.4 collective-permute-start.10
  425.9 9.4 %collective-permute-start.7 = (bf16[3,896,512]{2,1,0:T(8,128)(2,1)}, bf16[3,896,512]{2,1,0:T(8,128)(2,1)}, u32[]{:S(2)}, u32[]{:S(2)}) collective-permute-start(bf16[3,896,512]{2,1,0:T(8,128)(2,1)} %collective-permute-done.refs_6_), channel_id=1, source_target_pairs={{0,1},{1,0},{2,3},{3,2},{4,5},{5,4},{6,7},{7,6},{8,9},{9,8},{10,11... | collective-permute-start | bytes 8257544 | tf_op jit(solution)/shard_map/ppermute | solution.py:648
  426.4 12.8 %collective-permute-start.8 = (bf16[3,896,512]{2,1,0:T(8,128)(2,1)}, bf16[3,896,512]{2,1,0:T(8,128)(2,1)}, u32[]{:S(2)}, u32[]{:S(2)}) collective-permute-start(bf16[3,896,512]{2,1,0:T(8,128)(2,1)} %collective-permute-done.4.refs_8_), channel_id=1, source_target_pairs={{0,1},{1,0},{2,3},{3,2},{4,5},{5,4},{6,7},{7,6},{8,9},{9,8},{10,11... | collective-permute-start | bytes 8257544 | tf_op jit(solution)/shard_map/ppermute | solution.py:648
  426.5 16.7 %collective-permute-start.9 = (bf16[3,896,512]{2,1,0:T(8,128)(2,1)}, bf16[3,896,512]{2,1,0:T(8,128)(2,1)}, u32[]{:S(2)}, u32[]{:S(2)}) collective-permute-start(bf16[3,896,512]{2,1,0:T(8,128)(2,1)} %collective-permute-done.5.refs_10_), channel_id=1, source_target_pairs={{0,1},{1,0},{2,3},{3,2},{4,5},{5,4},{6,7},{7,6},{8,9},{9,8},{10,11... | collective-permute-start | bytes 8257544 | tf_op jit(solution)/shard_map/ppermute | solution.py:648
  431.2 11.9 %copy-start.13 = (bf16[3,896,512]{2,1,0:T(8,128)(2,1)}, bf16[3,896,512]{2,1,0:T(8,128)(2,1)S(1)}, u32[]{:S(2)}) copy-start(bf16[3,896,512]{2,1,0:T(8,128)(2,1)S(1)} %collective-permute-done.10.refs_13_) | copy-start | bytes 8257540
where the time goes:
time: 602 us; the launch traced here: 594 us
  Pallas kernels  455 us (76%)
  local copies, waits for them, and re-layouts  47.7 us (8%)
  other arithmetic  35.9 us (6%)
  matrix products  26.2 us (4%)
  starting transfers between devices  14.8 us (2%)
  waiting for transfers between devices  12.1 us (2%)
    pallas_call x1, Pallas kernels, reduce_call(): pl.pallas_call(functools.partial(reduce_body, zn, nt, tn, hr), out_shape=...  222 us
    pallas_call x1, Pallas kernels, mlp_call(): pl.pallas_call(functools.partial(mlp_body, zn, nq, hr, cw), out_shape=(ja...  142 us
    pallas_call x1, Pallas kernels, attend_call(): pl.pallas_call(functools.partial(attend_body, rows, nope, rope, scale), g...  90.5 us
    unnamed x39, local copies, waits for them, and re-layouts  14.8 us
    ppermute x4, waiting for transfers between devices, core_step(): out += [part, lax.ppermute(part, 'side', [(0, 1), (1, 0), (2, 3), (3, 2)])]  12.1 us
  transfers between devices with their start and end apart: 11, of which 4 were waited for; matrix products, arithmetic and copies ran while one was open for 15% of the time, Pallas kernels for 53%

commit v1 on v0

--- a/solution.py
+++ b/solution.py
@@ -9,6 +9,7 @@
 EPSILON = 1e-6
 THETA = 10000.0
 TOK_PAD = 8
+BITS = (1, 2, 4)
 dma = pltpu.SemaphoreType.DMA
 mesh_id = pl.DeviceIdType.MESH
 none = None
@@ -17,10 +18,8 @@
 MID_LAG = 2
 
 
-def rms_scaled(values, gain):
-    hidden = values.astype(jnp.float32)
-    inv_rms = lax.rsqrt(jnp.mean(hidden * hidden, axis=-1, keepdims=True) + EPSILON)
-    return (hidden * inv_rms * gain.astype(jnp.float32)).astype(jnp.bfloat16)
+def odd(value):
+    return lax.rem(value, 2)
 
 
 def rms_plain(values):
@@ -47,19 +46,20 @@
     return jnp.tile(jnp.cos(angles), (1, 4)), jnp.tile(jnp.sin(angles), (1, 4))
 
 
-def make_latent(normed, w_dkv_layer, positions, rank_dim):
-    latent_raw = jnp.dot(normed, w_dkv_layer, preferred_element_type=jnp.float32).astype(jnp.bfloat16)
+def finish_latent(latent_raw, positions, rank_dim):
     return jnp.concatenate([rms_plain(latent_raw[:, :rank_dim]), apply_rope(latent_raw[:, rank_dim:], positions)], axis=-1)
 
 
-def expand_latent(latent_pack, w_uk_layer, w_uv_layer):
+def expand_keys(latent_pack, w_uk_layer):
     rank_dim = w_uk_layer.shape[0]
-    latent = latent_pack[:, :rank_dim]
     rope_key = latent_pack[:, rank_dim:]
-    key_nope = jnp.einsum('sr,rhn->shn', latent, w_uk_layer, preferred_element_type=jnp.float32).astype(jnp.bfloat16)
-    value_full = jnp.einsum('sr,rhv->shv', latent, w_uv_layer, preferred_element_type=jnp.float32).astype(jnp.bfloat16)
+    key_nope = jnp.einsum('sr,rhn->shn', latent_pack[:, :rank_dim], w_uk_layer, preferred_element_type=jnp.float32).astype(jnp.bfloat16)
     rope_heads = jnp.broadcast_to(rope_key[:, None, :], (key_nope.shape[0], key_nope.shape[1], rope_key.shape[1]))
-    return jnp.concatenate([key_nope, rope_heads], axis=-1), value_full
+    return jnp.concatenate([key_nope, rope_heads], axis=-1)
+
+
+def expand_values(latent_pack, w_uv_layer):
+    return jnp.einsum('sr,rhv->shv', latent_pack[:, :w_uv_layer.shape[0]], w_uv_layer, preferred_element_type=jnp.float32).astype(jnp.bfloat16)
 
 
 def masked_softmax(scores, allowed):
@@ -94,6 +94,48 @@
     @pl.when((zi > 0) & (zi < zn - 1))
     def _():
         pl.semaphore_wait(sem, 2 + len(also))
+
+
+def latent_body(x_ref, t_ref, gain_ref, w_ref, n_ref, raw_ref, acc):
+    rows, depth = x_ref.shape
+    step = t_ref.shape[0]
+    chunk = depth // 4
+
+    def norm(x):
+        x = x.astype(jnp.float32)
+        inv = lax.rsqrt(jnp.mean(x * x, axis=-1, keepdims=True) + EPSILON)
+        return (x * inv * gain_ref[...]).astype(jnp.bfloat16)
+
+    @pl.loop(0, rows // step)
+    def _(r):
+        span = pl.ds(pl.multiple_of(r * step, step), step)
+        n_ref[span] = norm(x_ref[span])
+
+    n_ref[rows:] = norm(t_ref[...])
+    acc[...] = jnp.zeros_like(acc)
+
+    @pl.loop(0, 4)
+    def _(c):
+        span = pl.ds(pl.multiple_of(c * chunk, chunk), chunk)
+        acc[...] = acc[...] + lax.dot_general(n_ref[:, span], w_ref[:, span], (((1,), (1,)), ((), ())), preferred_element_type=jnp.float32)
+
+    raw_ref[...] = acc[...].astype(jnp.bfloat16)
+
+
+def latent_call(x_rows, t_rows, gain, w_dkv):
+    total = x_rows.shape[0] + t_rows.shape[0]
+    feat, depth = w_dkv.shape
+    vm = pl.BlockSpec(memory_space=pltpu.VMEM)
+    return pl.pallas_call(
+        latent_body,
+        out_shape=(jax.ShapeDtypeStruct((total, depth), jnp.bfloat16), jax.ShapeDtypeStruct((total, feat), jnp.bfloat16)),
+        in_specs=[vm] * 4,
+        out_specs=(vm, vm),
+        scratch_shapes=[pltpu.VMEM((total, feat), jnp.float32)],
+        compiler_params=pltpu.CompilerParams(vmem_limit_bytes=40_000_000),
+        cost_estimate=pl.CostEstimate(flops=2 * total * depth * feat, bytes_accessed=depth * (feat + 2 * total) * 2, transcendentals=0),
+        name='latent',
+    )(x_rows, t_rows, gain, w_dkv)
 
 
 def attend_body(rows, nope, rope, scale, n_ref, w_ref, k_ref, r_ref, v_ref, cos_ref, sin_ref, len_ref, o_ref, qt_ref, acc):
@@ -119,9 +161,10 @@
     valid = len_ref[0]
     kr = r_ref[...]
     half_rows = rows // 2
-    for pair in range(heads // 2):
-        base = pair * 2 * (nope + rope)
-        t0, t1, t2 = (acc[:, base + nope * i:base + nope * (i + 1)].astype(jnp.bfloat16).astype(jnp.float32) for i in range(3))
+
+    @pl.loop(0, heads // 2)
+    def _(pair):
+        t0, t1, t2 = (acc[:, pl.ds(pl.multiple_of((pair * 3 + i) * nope, nope), nope)].astype(jnp.bfloat16).astype(jnp.float32) for i in range(3))
         n1 = jnp.where(low, pltpu.roll(t1, rope, 1), pltpu.roll(t2, rope, 1))
         both = jnp.where(low, t1, t2)
         turned = jnp.where(first, -pltpu.roll(both, 2 * rope - rope // 2, 1), pltpu.roll(both, rope // 2, 1))
@@ -133,21 +176,21 @@
             qt_ref[h] = query[rows:]
             for blk in range(2):
                 span = (blk + 1) * half_rows
-                key = jnp.concatenate([k_ref[h, :, :span], kr[:, :span]], axis=0)
-                s = jnp.dot(query[blk * half_rows:(blk + 1) * half_rows], key, preferred_element_type=jnp.float32) * scale
+                key = jnp.concatenate([k_ref[h, :span], kr[:span]], axis=1)
+                s = lax.dot_general(query[blk * half_rows:(blk + 1) * half_rows], key, (((1,), (1,)), ((), ())), preferred_element_type=jnp.float32) * scale
                 row = lax.broadcasted_iota(jnp.int32, s.shape, 0) + blk * half_rows
                 col = lax.broadcasted_iota(jnp.int32, s.shape, 1)
                 s = jnp.where((col <= row) & (col < valid), s, -1e30)
                 p = jnp.exp(s - jnp.max(s, axis=1, keepdims=True))
                 p = (p * (1.0 / jnp.sum(p, axis=1, keepdims=True))).astype(jnp.bfloat16)
                 out = jnp.dot(p, v_ref[h, :span, :], preferred_element_type=jnp.float32)
-                o_ref[blk * half_rows:(blk + 1) * half_rows, h * nope:(h + 1) * nope] = out.astype(jnp.bfloat16)
-
-
-def attend_call(normed, w_q, key_t, rope_t, value, cos, sin, valid_len, rows, scale):
+                o_ref[blk * half_rows:(blk + 1) * half_rows, pl.ds(pl.multiple_of(h * nope, nope), nope)] = out.astype(jnp.bfloat16)
+
+
+def attend_call(normed, w_q, key_all, rope_two, value, cos, sin, valid_len, rows, scale):
     total, depth = normed.shape
     heads, feat, _ = w_q.shape
-    nope = key_t.shape[1]
+    nope = key_all.shape[2]
     rope = feat - nope
     vdim = value.shape[2]
     grp = 4
@@ -159,7 +202,7 @@
         in_specs=[
             vm,
             pl.BlockSpec((grp, feat, depth), lambda g: (g, 0, 0)),
-            pl.BlockSpec((grp, nope, key_t.shape[2]), lambda g: (g, 0, 0)),
+            pl.BlockSpec((grp, key_all.shape[1], nope), lambda g: (g, 0, 0)),
             vm,
             pl.BlockSpec((grp, value.shape[1], vdim), lambda g: (g, 0, 0)),
             vm, vm,
@@ -170,14 +213,14 @@
         compiler_params=pltpu.CompilerParams(vmem_limit_bytes=60_000_000),
         cost_estimate=pl.CostEstimate(flops=2 * total * depth * heads * feat + 3 * rows * rows * heads * feat, bytes_accessed=heads * feat * depth * 2, transcendentals=rows * rows * heads),
         name='attend',
-    )(normed, w_q, key_t, rope_t, value, cos, sin, valid_len)
-
-
-def reduce_body(zn, nt, tn, hr, p_ref, q_ref, x_ref, t_ref, w_ref, m2_ref, m3_ref, o_ref, ot_ref, g_ref, a_ref, asem, gs, gr, wbuf, pdn, pup, rdn, rup, wsem, sdn, sup, vdn, vup):
+    )(normed, w_q, key_all, rope_two, value, cos, sin, valid_len)
+
+
+def reduce_body(zn, nt, tn, hr, p_ref, q_ref, x_ref, t_ref, w_ref, f0_ref, f1_ref, f2_ref, f3_ref, m2_ref, m3_ref, o_ref, ot_ref, g_ref, xc_ref, a_ref, asem, gs, gr, xs, xr, wbuf, pdn, pup, rdn, rup, wsem, sdn, sup, vdn, vup):
     zi = lax.axis_index('tp')
 
     def wcopy(j):
-        return pltpu.make_async_copy(w_ref.at[:, pl.ds(pl.multiple_of(j * tn, 128), tn)], wbuf.at[lax.rem(j, 2)], wsem.at[lax.rem(j, 2)])
+        return pltpu.make_async_copy(w_ref.at[:, pl.ds(pl.multiple_of(j * tn, 128), tn)], wbuf.at[odd(j)], wsem.at[odd(j)])
 
     def send_dn(i):
         return pltpu.make_async_remote_copy(pdn.at[i], rdn.at[i], sdn.at[i], vdn.at[i], device_id={'tp': zi - 1}, device_id_type=mesh_id)
@@ -201,6 +244,20 @@
             src, dst = g_ref.at[k, 1, :, pl.ds(cut, cut)], g_ref.at[k, 2, :, pl.ds(cut, cut)]
         return pltpu.make_async_remote_copy(src, dst, gs.at[k, c], gr.at[k, c], device_id=(over_y, over_x, over_x, over_y)[c], device_id_type=mesh_id)
 
+    side = lax.axis_index('side')
+    partner = {'side': side + 1 - 2 * odd(side)}
+
+    def cross(k, c):
+        if k == 0:
+            src = (f0_ref, f1_ref, f2_ref, f3_ref)[c]
+        elif c == 0:
+            src = (m2_ref, m3_ref)[k - 1]
+        else:
+            src = g_ref.at[k - 1, c - 1]
+        return pltpu.make_async_remote_copy(src, xc_ref.at[k, c], xs.at[k, c], xr.at[k, c], device_id=partner, device_id_type=mesh_id)
+
+    crossed = [(k, c) for k in range(3) for c in range(4) if k + c < 5]
+
     wcopy(0).start()
     fill = [
         pltpu.make_async_copy(p_ref, a_ref.at[pl.ds(0, 2 * hr)], asem.at[0]),
@@ -208,13 +265,16 @@
     ]
     for one in fill:
         one.start()
-    line_barrier(zi, zn, (over_y, over_x))
+    line_barrier(zi, zn, (over_y, over_x, partner))
 
     @pl.when(ends)
     def _():
         for k in range(2):
             for c in range(2):
                 plane(k, c).start()
+        for k, c in crossed:
+            if k * c == 0:
+                cross(k, c).start()
 
     for one in fill:
         one.wait()
@@ -276,7 +336,7 @@
         def _():
             wcopy(j + 1).start()
 
-        wt = wbuf[lax.rem(j, 2)]
+        wt = wbuf[odd(j)]
         part = jnp.dot(a_ref[...], wt, preferred_element_type=jnp.float32)
         pdn[j, :hr] = part[:hr]
         pdn[j, hr:] = part[2 * hr:2 * hr + TOK_PAD]
@@ -301,6 +361,8 @@
                 plane(k, 1).wait_recv()
                 plane(k, 2).start()
                 plane(k, 3).start()
+                cross(k + 1, 1).start()
+                cross(k + 1, 2).start()
 
     @pl.loop(nt - lag, nt + 1)
     def _(j):
@@ -321,11 +383,15 @@
         for k in range(2):
             plane(k, 2).wait_recv()
             plane(k, 3).wait_recv()
+            if k == 0:
+                cross(1, 3).start()
             for c in range(4):
                 plane(k, c).wait_send()
-
-
-def reduce_call(p_rows, q_rows, x_own, t_own, w_o, m2, m3, zn):
+        for k, c in crossed:
+            cross(k, c).wait()
+
+
+def reduce_call(p_rows, q_rows, x_own, t_own, w_o, first, m2, m3, zn):
     hr, width = x_own.shape
     depth = p_rows.shape[1]
     total = p_rows.shape[0] + q_rows.shape[0]
@@ -340,14 +406,14 @@
             jax.ShapeDtypeStruct((hr, width), jnp.bfloat16),
             jax.ShapeDtypeStruct((TOK_PAD, width), jnp.float32),
             jax.ShapeDtypeStruct((2, 3) + m2.shape, jnp.bfloat16),
+            jax.ShapeDtypeStruct((3, 4) + m2.shape, jnp.bfloat16),
         ),
-        in_specs=[hb, hb, vm, vm, hb, hb, hb],
-        out_specs=(vm, vm, hb),
+        in_specs=[hb, hb, vm, vm] + [hb] * 7,
+        out_specs=(vm, vm, hb, hb),
         scratch_shapes=[
             pltpu.VMEM((total, depth), jnp.bfloat16),
             dma((2,)),
-            dma((2, 4)),
-            dma((2, 4)),
+            *[dma((n, 4)) for n in (2, 2, 3, 3)],
             pltpu.VMEM((2, depth, tn), jnp.bfloat16),
             pltpu.VMEM((nt, td, tn), jnp.float32),
             pltpu.VMEM((nt, hr, tn), jnp.float32),
@@ -362,56 +428,55 @@
         compiler_params=pltpu.CompilerParams(collective_id=0, has_side_effects=True, vmem_limit_bytes=66_000_000),
         cost_estimate=pl.CostEstimate(flops=2 * total * depth * width, bytes_accessed=depth * width * 2, transcendentals=0),
         name='wo_reduce',
-    )(p_rows, q_rows, x_own, t_own, w_o, m2, m3)
+    )(p_rows, q_rows, x_own, t_own, w_o, *first, m2, m3)
 
 
 def mlp_body(zn, nq, hr, cw, *refs):
-    b_ref, h_ref, t_ref, wg_ref, wu_ref, wd_ref = refs[:6]
+    h_ref, t_ref, gain_ref, wg_ref, wu_ref, wd_ref = refs[:6]
     half = nq // 2
-    n_in = nq + 3
-    pieces = refs[6:6 + nq]
-    plane_own, spread = refs[6 + nq:8 + nq], refs[8 + nq]
-    o_ref, ot_ref, xc_ref, gacc, uacc, m_ref, wbuf, obuf, dbuf, wsem, dsem, xs, xr, sa, ra, sb, rb, st, rt = refs[6 + n_in:]
+    n_in = half + 4
+    first = refs[6:6 + half]
+    plane_own = refs[6 + half:8 + half]
+    spread, crossed = refs[8 + half:6 + n_in]
+    o_ref, ot_ref, xl_ref, b_ref, gacc, uacc, m_ref, wbuf, obuf, dbuf, wsem, dsem, xs, xr, sa, ra, sb, rb, st, rt = refs[6 + n_in:]
     zi = lax.axis_index('tp')
     side = lax.axis_index('side')
     qi = lax.axis_index('pair') * (nq // 2) + side
     slots = 4
-    steps = slots * nq
-    depth = 4
+    depth = wbuf.shape[0]
 
     def flip(e):
         out = 0
-        for bit in (1, 2, 4):
-            out = out + bit * lax.rem(lax.rem(qi // bit, 2) + lax.rem(e // bit, 2), 2)
+        for bit in BITS:
+            out = out + bit * odd(lax.rem(qi // bit, 2) + lax.rem(e // bit, 2))
         return out
 
     def cols_at(q):
         return pl.ds(pl.multiple_of(q * cw, 128), cw)
 
-    order = [(s, e) for s in (0, 1) for e in range(nq)]
-    order += [(s, e) for par in (0, 1) for s in (2, 3) for e in range(par, nq, 2)]
-
-    def slot_piece(i):
-        late = i - 2 * nq
-        early = i < 2 * nq
-        s = jnp.where(early, i // nq, 2 + lax.rem(late // half, 2))
-        e = jnp.where(early, lax.rem(i, nq), 2 * lax.rem(late, half) + late // (2 * half))
-        return s, e
-
-    partner = {'side': side + 1 - 2 * lax.rem(side, 2)}
+    two = range(2)
+    order = [(s, e, e + 1) for s in two for e in range(0, nq, 2)]
+    order += [(s + 2, e, e + 2) for par in two for s in two for e in range(par, nq, 4)]
+    steps = len(order)
+
+    def slot_pieces(i):
+        late = i - nq
+        early = i < nq
+        s = jnp.where(early, i // half, 2 + odd(late // 2))
+        ea = jnp.where(early, 2 * lax.rem(i, half), 4 * odd(late) + late // half)
+        return s, ea, ea + jnp.where(early, 1, 2)
+
+    partner = {'side': side + 1 - 2 * odd(side)}
 
     def at_hand(k, j):
         return plane_own[k] if j == 0 else spread.at[k, j - 1]
 
-    def cross(k, j):
-        return pltpu.make_async_remote_copy(at_hand(k, j), xc_ref.at[k, j], xs.at[k, j], xr.at[k, j], device_id=partner, device_id_type=mesh_id)
+    last = pltpu.make_async_remote_copy(at_hand(1, half - 1), xl_ref, xs, xr, device_id=partner, device_id_type=mesh_id)
 
     def source(s, e):
-        if s == 1:
-            return pieces[e]
-        if e % 2 == 0:
-            return at_hand(s - 2, e // 2)
-        return xc_ref.at[s - 2, e // 2]
+        if e % 2:
+            return xl_ref if (s, e) == (slots - 1, nq - 1) else crossed.at[s - 1, e // 2]
+        return first[e // 2] if s == 1 else at_hand(s - 2, e // 2)
 
     line_barrier(zi, zn, (partner,))
     ends = (zi == 0) | (zi == zn - 1)
@@ -419,27 +484,29 @@
     def start_gu(i):
         buf = lax.rem(i, depth)
 
-        @pl.when(i < nq)
-        def _():
-            rows = cols_at(flip(i))
-            pltpu.make_async_copy(wg_ref.at[rows, :], wbuf.at[buf, 0], wsem.at[buf]).start()
-            pltpu.make_async_copy(wu_ref.at[rows, :], wbuf.at[buf, 1], wsem.at[buf]).start()
-
-        for k, (s, e) in enumerate(order):
+        @pl.when(i < half)
+        def _():
+            for h in two:
+                rows = cols_at(flip(2 * i + h))
+                pltpu.make_async_copy(wg_ref.at[rows, :], wbuf.at[buf, 0, pl.ds(h * cw, cw)], wsem.at[buf]).start()
+                pltpu.make_async_copy(wu_ref.at[rows, :], wbuf.at[buf, 1, pl.ds(h * cw, cw)], wsem.at[buf]).start()
+
+        for k, (s, *es) in enumerate(order):
             if s > 0:
                 @pl.when(i == k)
-                def _(s=s, e=e):
-                    if s > 1 and e % 2:
-                        cross(s - 2, e // 2).wait_recv()
-                    pltpu.make_async_copy(source(s, e).at[pl.ds(0, 2)], wbuf.at[buf], wsem.at[buf]).start()
+                def _(s=s, es=es):
+                    for h, e in enumerate(es):
+                        if (s, e) == (slots - 1, nq - 1):
+                            last.wait_recv()
+                        pltpu.make_async_copy(source(s, e).at[pl.ds(0, 2)], wbuf.at[buf, :, pl.ds(h * cw, cw)], wsem.at[buf]).start()
 
     def start_dn(e):
-        pltpu.make_async_copy(wd_ref.at[:, cols_at(flip(e))], obuf.at[lax.rem(e, 2)], dsem.at[lax.rem(e, 2), 0]).start()
+        pltpu.make_async_copy(wd_ref.at[:, cols_at(flip(e))], obuf.at[odd(e)], dsem.at[odd(e), 0]).start()
         for k in range(nq):
             @pl.when(e == k)
             def _(k=k):
                 for s in range(1, slots):
-                    pltpu.make_async_copy(source(s, k).at[2], dbuf.at[lax.rem(e, 2), s - 1], dsem.at[lax.rem(e, 2), s]).start()
+                    pltpu.make_async_copy(source(s, k).at[2], dbuf.at[odd(e), s - 1], dsem.at[odd(e), s]).start()
 
     hh = hr // 2
 
@@ -458,25 +525,34 @@
 
     @pl.when(ends)
     def _():
-        for k in range(2):
-            for j in range(half):
-                cross(k, j).start()
+        last.start()
         for i in range(depth - 1):
             start_gu(jnp.int32(i))
+
+        def norm(x):
+            inv = lax.rsqrt(jnp.mean(x * x, axis=-1, keepdims=True) + EPSILON)
+            return (x * inv * gain_ref[...]).astype(jnp.bfloat16)
+
+        @pl.loop(0, hr // 16)
+        def _(r):
+            span = pl.ds(pl.multiple_of(r * 16, 16), 16)
+            b_ref[span] = norm(h_ref[span].astype(jnp.float32))
+
+        b_ref[hr:] = norm(jnp.concatenate([t_ref[...]] * 2, axis=0))
         gacc[...] = jnp.zeros_like(gacc)
         uacc[...] = jnp.zeros_like(uacc)
 
         @pl.loop(0, steps)
         def _(i):
             buf = lax.rem(i, depth)
-            s, e = slot_piece(i)
-            pltpu.make_async_copy(pieces[0].at[pl.ds(0, 2)], wbuf.at[buf], wsem.at[buf]).wait()
+            s, ea, eb = slot_pieces(i)
+            pltpu.make_async_copy(wbuf.at[buf], wbuf.at[buf], wsem.at[buf]).wait()
 
             @pl.when(i + depth - 1 < steps)
             def _():
                 start_gu(i + depth - 1)
 
-            rows = b_ref[:, cols_at(flip(e))]
+            rows = jnp.concatenate([b_ref[:, cols_at(flip(ea))], b_ref[:, cols_at(flip(eb))]], axis=1)
             gacc[s] = gacc[s] + jnp.dot(rows, wbuf[buf, 0], preferred_element_type=jnp.float32)
             uacc[s] = uacc[s] + jnp.dot(rows, wbuf[buf, 1], preferred_element_type=jnp.float32)
 
@@ -489,7 +565,7 @@
 
         @pl.loop(0, nq)
         def _(e):
-            par = lax.rem(e, 2)
+            par = odd(e)
             q = flip(e)
             cols = cols_at(q)
 
@@ -499,7 +575,7 @@
 
             acc = None
             for s in range(slots):
-                pltpu.make_async_copy(pieces[0].at[2], dbuf.at[par, max(s - 1, 0)], dsem.at[par, s]).wait()
+                pltpu.make_async_copy(first[0].at[2], dbuf.at[par, max(s - 1, 0)], dsem.at[par, s]).wait()
                 if s == 0:
                     acc = jnp.dot(m_ref[s], obuf[par], preferred_element_type=jnp.float32)
                 else:
@@ -510,19 +586,17 @@
             def _():
                 o_ref[:hr, cols] = res
                 ot_ref[:, cols] = (t_ref[:, cols].astype(jnp.bfloat16) + acc[hr:hr + TOK_PAD].astype(jnp.bfloat16)).astype(jnp.float32)
-                up(q, 0).start()
-                up(q, 1).start()
+                for r in two:
+                    up(q, r).start()
                 tok(q).start()
 
             @pl.when(zi == zn - 1)
             def _():
                 o_ref[hr:, cols] = res
-                down(q, 0).start()
-                down(q, 1).start()
-
-        for k in range(2):
-            for j in range(half):
-                cross(k, j).wait_send()
+                for r in two:
+                    down(q, r).start()
+
+        last.wait_send()
 
     @pl.when((zi > 0) & (zi < zn - 1))
     def _():
@@ -530,18 +604,18 @@
         def _(i):
             def pass_up(n):
                 q = flip(n // 2)
-                up(q, lax.rem(n, 2)).wait_recv()
-                up(q, lax.rem(n, 2)).start()
-
-                @pl.when(lax.rem(n, 2) == 1)
+                up(q, odd(n)).wait_recv()
+                up(q, odd(n)).start()
+
+                @pl.when(odd(n) == 1)
                 def _():
                     tok(q).wait_recv()
                     tok(q).start()
 
             def pass_down(n):
                 q = flip(n // 2)
-                down(q, lax.rem(n, 2)).wait_recv()
-                down(q, lax.rem(n, 2)).start()
+                down(q, odd(n)).wait_recv()
+                down(q, odd(n)).start()
 
             def ordered(near, far):
                 @pl.when(i < 2 * nq)
@@ -564,31 +638,31 @@
     def _(q):
         @pl.when(zi == zn - 1)
         def _():
-            up(q, 0).wait_recv()
-            up(q, 1).wait_recv()
+            for r in two:
+                up(q, r).wait_recv()
             tok(q).wait_recv()
 
         @pl.when(zi == 0)
         def _():
-            down(q, 0).wait_recv()
-            down(q, 1).wait_recv()
+            for r in two:
+                down(q, r).wait_recv()
 
         @pl.when(zi < zn - 1)
         def _():
-            up(q, 0).wait_send()
-            up(q, 1).wait_send()
+            for r in two:
+                up(q, r).wait_send()
             tok(q).wait_send()
 
         @pl.when(zi > 0)
         def _():
-            down(q, 0).wait_send()
-            down(q, 1).wait_send()
-
-
-def mlp_call(b_rows, h_rows, t_rows, w_gate, w_up, w_down, pieces, zn):
+            for r in two:
+                down(q, r).wait_send()
+
+
+def mlp_call(h_rows, t_rows, gain, w_gate, w_up, w_down, pieces, zn):
     hr, width = h_rows.shape
-    br = b_rows.shape[0]
-    nq = len(pieces) - 3
+    br = hr + 2 * TOK_PAD
+    nq = 2 * (len(pieces) - 4)
     fw = w_gate.shape[1]
     cw = width // nq
     vm = pl.BlockSpec(memory_space=pltpu.VMEM)
@@ -598,26 +672,27 @@
         out_shape=(
             jax.ShapeDtypeStruct((2 * hr, width), jnp.bfloat16),
             jax.ShapeDtypeStruct((TOK_PAD, width), jnp.float32),
-            jax.ShapeDtypeStruct((2, nq // 2, 3, cw, fw), jnp.bfloat16),
+            jax.ShapeDtypeStruct((3, cw, fw), jnp.bfloat16),
         ),
         in_specs=[vm, vm, vm] + [hb] * (3 + len(pieces)),
         out_specs=(vm, vm, hb),
         scratch_shapes=[
+            pltpu.VMEM((br, width), jnp.bfloat16),
             pltpu.VMEM((4, br, fw), jnp.float32),
             pltpu.VMEM((4, br, fw), jnp.float32),
             pltpu.VMEM((4, br, fw), jnp.bfloat16),
-            pltpu.VMEM((4, 2, cw, fw), jnp.bfloat16),
+            pltpu.VMEM((3, 2, 2 * cw, fw), jnp.bfloat16),
             pltpu.VMEM((2, fw, cw), jnp.bfloat16),
             pltpu.VMEM((2, 3, cw, fw), jnp.bfloat16),
-            dma((4,)),
+            dma((3,)),
             dma((2, 4)),
-            dma((2, nq // 2)),
-            dma((2, nq // 2)),
+            dma,
+            dma,
         ] + [dma((2, nq)) for _ in range(4)] + [dma((nq,)) for _ in range(2)],
         compiler_params=pltpu.CompilerParams(collective_id=1, has_side_effects=True, vmem_limit_bytes=60_000_000),
         cost_estimate=pl.CostEstimate(flops=2 * br * 4 * fw * width * 3, bytes_accessed=4 * fw * width * 6, transcendentals=0),
         name='mlp_spread',
-    )(b_rows, h_rows, t_rows, w_gate, w_up, w_down, *pieces)
+    )(h_rows, t_rows, gain, w_gate, w_up, w_down, *pieces)
     return out[0], out[1]
 
 
@@ -636,17 +711,10 @@
 
 
 def plane_step(mine):
-    over_y = lax.ppermute(mine, 'side', [(0, 2), (2, 0), (1, 3), (3, 1)])
-    over_x = lax.ppermute(mine, 'pair', [(0, 1), (1, 0)])
+    over_y = lax.ppermute(mine, 'side', [(c, c ^ 2) for c in range(4)])
+    over_x = lax.ppermute(mine, 'pair', [(p, 1 - p) for p in range(2)])
     over_d = lax.ppermute(mine, ('pair', 'side'), [(p * 4 + s, (1 - p) * 4 + (s + 2) % 4) for p in range(2) for s in range(4)])
     return [mine, over_y, over_x, over_d]
-
-
-def core_step(parts):
-    out = []
-    for part in parts:
-        out += [part, lax.ppermute(part, 'side', [(0, 1), (1, 0), (2, 3), (3, 2)])]
-    return out
 
 
 def tie(*values):
@@ -678,29 +746,30 @@
         own = own_piece(w_gate, w_up, w_down, nq)
         near = to_ends(own, 1, zn)
 
-        every = jnp.concatenate([hidden, toks, jnp.zeros((16 - nb, width), hidden.dtype)], axis=0)
+        some = jnp.concatenate([toks, jnp.zeros((16 - nb, width), toks.dtype)], axis=0)
         positions = jnp.concatenate([jnp.arange(rows, dtype=jnp.int32), cur_len, jnp.zeros((16 - nb,), jnp.int32)])
-        normed = rms_scaled(every, attn_gain)
-        latent_pack = make_latent(normed, w_dkv, positions, w_uk.shape[0])
+        normed, latent_raw = latent_call(hidden, some, attn_gain[None].astype(jnp.float32), w_dkv.T)
+        latent_pack = finish_latent(latent_raw, positions, w_uk.shape[0])
         received = lax.ppermute(latent_pack[:rows], 'side', shift_pairs)
         nope, rank = w_uk.shape[-1], w_uk.shape[0]
         heads, rope = w_q.shape[1], w_q.shape[2] - nope
         latent, rope_key = latent_pack[:, :rank], latent_pack[:, rank:]
-        key_t = jnp.einsum('sr,rhn->hns', latent, w_uk, preferred_element_type=jnp.float32).astype(jnp.bfloat16)
+        key_all = jnp.einsum('sr,rhn->hsn', latent, w_uk, preferred_element_type=jnp.float32).astype(jnp.bfloat16)
         value = jnp.einsum('sr,rhv->hsv', latent, w_uv, preferred_element_type=jnp.float32).astype(jnp.bfloat16)
         cos, sin = rope_tables(positions, rope)
-        rope_t = jnp.concatenate([rope_key[:rows].T] * 2, axis=0)
-        normed, own, near = tie(normed, own, near)
+        rope_two = jnp.concatenate([rope_key[:rows]] * 2, axis=1)
+        normed, own, near, later = tie(normed, own, near, received)
         first = plane_step(near)
         middle = to_ends(own, 2, zn)
         far = to_ends(own, 3, zn)
-        p_rows, q_tok = attend_call(normed, w_q.transpose(1, 2, 0), key_t, rope_t, value, cos, sin, s_len, rows, w_q.shape[2] ** -0.5)
-
+        p_rows, q_tok = attend_call(normed, w_q.transpose(1, 2, 0), key_all, rope_two, value, cos, sin, s_len, rows, w_q.shape[2] ** -0.5)
+
+        rope_new = jnp.broadcast_to(rope_key[rows:rows + nb, None, :], (nb, heads, rope))
+        key_new = jnp.concatenate([key_all[:, rows:rows + nb].transpose(1, 0, 2), rope_new], axis=-1)
+        value_new = value[:, rows:rows + nb].transpose(1, 0, 2)
+        key_new, value_new, q_tok = tie(key_new, value_new, q_tok)
         q_rope = q_tok[:, :nb, nope:nope + rope] + q_tok[:, :nb, nope + rope:]
         query_tok = jnp.concatenate([q_tok[:, :nb, :nope], q_rope], axis=-1).transpose(1, 0, 2)
-        rope_new = jnp.broadcast_to(rope_key[rows:rows + nb, None, :], (nb, heads, rope))
-        key_new = jnp.concatenate([key_t[:, :, rows:rows + nb].transpose(2, 0, 1), rope_new], axis=-1)
-        value_new = value[:, rows:rows + nb].transpose(1, 0, 2)
         key_old, value_old = k_cache[0, 0], v_cache[0, 0]
         slot_hit = (jnp.arange(key_old.shape[1])[None, :] == cur_len[:, None])[:, :, None, None]
         key_layer = jnp.where(slot_hit, key_new[:, None], key_old)
@@ -708,21 +777,15 @@
         tok_val = cache_attention(query_tok, key_layer, value_layer, cur_len).reshape(nb, -1)
         q_rows = jnp.concatenate([tok_val, jnp.zeros((16 - nb, tok_val.shape[1]), tok_val.dtype)], axis=0)
 
-        p_rows, received = tie(p_rows, received)
         x_own = lax.dynamic_slice_in_dim(hidden, jnp.where(zi < zn // 2, 0, hr), hr, 0)
         t_own = jnp.concatenate([toks, jnp.zeros((TOK_PAD - nb, width), toks.dtype)], axis=0).astype(jnp.float32)
-        h_mid, t_mid, spread = reduce_call(p_rows, q_rows, x_own, t_own, w_o.reshape(-1, width), middle, far, zn)
-        h_mid, first = tie(h_mid, first)
-        pieces = core_step(first) + [middle, far, spread]
-
-        key_in, value_in = expand_latent(received, w_uk, w_uv)
-
-        b_rows = jnp.concatenate([
-            rms_scaled(h_mid, mlp_gain),
-            rms_scaled(t_mid.astype(jnp.bfloat16), mlp_gain),
-            jnp.zeros((TOK_PAD, width), jnp.bfloat16),
-        ], axis=0)
-        h_out, t_out = mlp_call(b_rows, h_mid, t_mid, w_gate, w_up, w_down, pieces, zn)
+        h_mid, t_mid, spread, crossed = reduce_call(p_rows, q_rows, x_own, t_own, w_o.reshape(-1, width), first, middle, far, zn)
+        pieces = [*first, middle, far, spread, crossed]
+
+        key_in = expand_keys(received, w_uk)
+        value_in = expand_values(later, w_uv)
+
+        h_out, t_out = mlp_call(h_mid, t_mid, mlp_gain[None].astype(jnp.float32), w_gate, w_up, w_down, pieces, zn)
         y_out = t_out[:nb].astype(jnp.bfloat16)
         return (h_out[None], y_out[None], key_in[None, None], value_in[None, None], key_layer[None, None], value_layer[None, None])
 

time: 602 us -> 528 us (0.88); the launches traced: 594 us -> 527 us
  Pallas kernels: 455 us -> 432 us
  other arithmetic: 35.9 us -> 16.1 us
  local copies, waits for them, and re-layouts: 47.7 us -> 38.1 us
  matrix products: 26.2 us -> 19.9 us
  waiting for transfers between devices: 12.1 us -> 5.92 us
    pallas_call x1, Pallas kernels: 222 us -> 193 us  [reduce_call(): pl.pallas_call(functools.partial(reduce_body, zn, nt, tn, hr), out_shape=...]
    pallas_call x0 -> x1, Pallas kernels: none -> 17.2 us  [latent_call(): pl.pallas_call(latent_body, out_shape=(jax.ShapeDtypeStruct((total, depth...]
    pallas_call x1, Pallas kernels: 142 us -> 129 us  [mlp_call(): pl.pallas_call(functools.partial(mlp_body, zn, nq, hr, cw), out_shape=(ja...]
    ppermute x6 -> x2, waiting for transfers between devices: 12.1 us -> 0.01 us  [the longest x1 0.01 us: plane_step(): over_y = lax.ppermute(mine, 'side', [(c, c ^ 2) for c in range(4)])]
    convert_element_type x1 -> x0, local copies, waits for them, and re-layouts: 8.83 us -> none  [device_step(): jnp.einsum('sr,rhn->hns', latent, w_uk, preferred_element_type=jnp.float32)]
    convert_element_type x4 -> x3, other arithmetic: 9.35 us -> 1.3 us  [the longest x1 0.64 us: device_step(): mlp_gain[None].astype(jnp.float32)]
    reduce_sum x3 -> x0, other arithmetic: 6.69 us -> none  [rms_scaled(): jnp.mean(hidden * hidden, axis=-1, keepdims=True) + EPSILON]
    dot_general x3 -> x2, matrix products: 15.7 us -> 9.71 us  [the longest x1 5.01 us: device_step(): jnp.einsum('sr,rhn->hsn', latent, w_uk, preferred_element_type=jnp.float32)]
  transfers between devices with their start and end apart: 11 -> 7, of which waited for: 4 -> 2; matrix products, arithmetic and copies ran while one was open for 15% -> 11% of each run, Pallas kernels for 53% -> 21%
where the time goes in v1:
time: 528 us; the launch traced here: 527 us
  Pallas kernels  432 us (82%)
  local copies, waits for them, and re-layouts  38.1 us (7%)
  matrix products  19.9 us (4%)
  other arithmetic  16.1 us (3%)
  starting transfers between devices  13.4 us (3%)
  waiting for transfers between devices  5.92 us (1%)
    pallas_call x1, Pallas kernels, reduce_call(): pl.pallas_call(functools.partial(reduce_body, zn, nt, tn, hr), out_shape=...  193 us
    pallas_call x1, Pallas kernels, mlp_call(): pl.pallas_call(functools.partial(mlp_body, zn, nq, hr, cw), out_shape=(ja...  129 us
    pallas_call x1, Pallas kernels, attend_call(): pl.pallas_call(functools.partial(attend_body, rows, nope, rope, scale), g...  92.6 us
    pallas_call x1, Pallas kernels, latent_call(): pl.pallas_call(latent_body, out_shape=(jax.ShapeDtypeStruct((total, depth...  17.2 us
    unnamed x27, local copies, waits for them, and re-layouts  15.8 us
  transfers between devices with their start and end apart: 7, of which 2 were waited for; matrix products, arithmetic and copies ran while one was open for 11% of the time, Pallas kernels for 21%

profile of v1, /device:TPU:0, one launch (start us, length us, event | category | flops | bytes accessed | tf_op | source)
XLA Modules:
  0.0 527.2 jit_solution(15638765045875424767)
XLA Ops:
  0.6 1.3 constant_dynamic-slice_fusion
  1.9 0.5 copy.82
  2.5 0.0 copy-start.6
  2.5 0.0 copy-start
  2.5 1.7 constant_dynamic-slice_fusion.1
  4.2 1.8 pad_maximum_fusion
  6.1 1.4 collective-permute-start
  7.6 0.0 copy-start.9
  7.6 17.2 %latent.1 = (bf16[528,7168]{1,0:T(8,128)(2,1)S(1)}, bf16[528,576]{1,0:T(8,128)(2,1)S(1)}) custom-call(bf16[512,7168]{1,0:T(8,128)(2,1)S(1)} %bitcast.70, bf16[16,7168]{1,0:T(8,128)(2,1)S(1)} %concatenate.40.t_ref, f32[1,7168]{1,0:T(1,128)S(1)} %convert_element_type.53.gain_ref, bf16[576,7168]{1,0:T(8,128)(2,1)} %bitcast.88), custom_call_target="tpu_custom_call" | custom-call | flops 4359979008 | bytes 23396352 | tf_op jit(solution)/shard_map/latent/pallas_call | solution.py:129
  24.9 3.0 copy-done.1
  27.8 0.2 fusion.19
  28.0 0.2 fusion.20
  28.3 0.1 add_convert_fusion
  28.3 1.1 fusion.26
  29.5 0.1 pad_maximum_fusion.1
  29.6 0.2 copy.83
  29.8 0.7 collective-permute-start.1
  30.6 0.1 fusion.29
  30.7 0.1 pad_maximum_fusion.5
  30.8 0.1 iota_compare_fusion.1
  30.8 0.8 pad_maximum_fusion.3.r_ref
  31.6 7.5 %copy.93 = bf16[512,32,128]{0,2,1:T(8,128)(2,1)} copy(bf16[512,32,128]{2,1,0:T(8,128)(2,1)} %bitcast.77) | data formatting | bytes 8388608 | tf_op jit(solution)/shard_map/squeeze | solution.py:739
  39.1 5.0 convert_bitcast_fusion.1.k_ref
  44.1 0.0 copy-start.10
  44.1 4.7 convert_bitcast_fusion.v_ref
  48.9 0.1 copy.86
  49.1 0.8 copy.88.cos_ref
  49.9 0.1 copy.87
  50.1 0.8 copy.89.sin_ref
  51.6 0.6 convert_element_type.66.refs_2_
  52.2 1.0 slice_bitcast_fusion.2
  53.2 4.4 dynamic-slice_bitcast_fusion.x_ref
  57.6 0.7 pad_convert_fusion.t_ref
  58.3 2.3 fusion.23
  60.7 0.6 convert_element_type.67
  61.3 0.2 broadcast_in_dim.102
  61.6 3.1 maximum_bitcast_fusion
  64.7 5.8 %collective-permute-done.f0_ref.refs_6_ = bf16[3,896,512]{2,1,0:T(8,128)(2,1)} collective-permute-done((bf16[3,896,512]{2,1,0:T(8,128)(2,1)}, bf16[3,896,512]{2,1,0:T(8,128)(2,1)}, u32[]{:S(2)}, u32[]{:S(2)}) %collective-permute-start) | collective-permute-done | bytes 2752544 | tf_op jit(solution)/shard_map/ppermute | solution.py:710
  70.5 2.3 collective-permute-start.2
  72.8 1.5 collective-permute-start.3
  74.3 1.3 collective-permute-start.5
  75.6 6.2 %collective-permute-start.6 = (bf16[3,896,512]{2,1,0:T(8,128)(2,1)}, bf16[3,896,512]{2,1,0:T(8,128)(2,1)}, u32[]{:S(2)}, u32[]{:S(2)}) collective-permute-start(bf16[3,896,512]{2,1,0:T(8,128)(2,1)} %pad_maximum_fusion), channel_id=1, source_target_pairs={{12,0},{0,12},{13,1},{1,13},{14,2},{2,14},{15,3},{3,15},{28,16},{1... | collective-permute-start | bytes 8257544 | tf_op jit(solution)/shard_map/ppermute | solution.py:710
  81.8 0.0 copy-start.3
  81.8 92.6 %attend.1 = (bf16[512,4096]{1,0:T(8,128)(2,1)}, bf16[32,16,256]{2,1,0:T(8,128)(2,1)}) custom-call(bf16[528,7168]{1,0:T(8,128)(2,1)} %copy-done.1, bf16[32,192,7168]{2,1,0:T(8,128)(2,1)} %bitcast.9.w_ref, bf16[32,528,128]{2,1,0:T(8,128)(2,1)} %copy-done.10, bf16[512,128]{1,0:T(8,128)(2,1)} %pad_maximum_fusion.3.r_ref, ...), custom_call_target="tpu_custom_call" | custom-call | flops 51338280960 | bytes 88080384 | tf_op jit(solution)/shard_map/attend/pallas_call | solution.py:198
  174.4 0.5 bitcast_select_fusion
  174.9 0.0 copy-start.5
  174.9 1.1 slice_add_fusion
  176.1 0.9 slice.57
  177.0 2.4 fusion.2
  179.4 0.2 fusion.18
  179.6 0.7 bitcast_select_fusion.1
  180.3 0.7 fusion.12
  181.1 0.7 concatenate.49.q_ref
  181.7 0.3 copy.94
  182.0 4.7 convert_bitcast_fusion.2
  186.8 4.7 copy.98
  191.5 1.5 broadcast_select_fusion.1
  193.0 1.4 copy-done.4
  194.4 2.2 broadcast_select_fusion
  196.7 0.1 collective-permute-done.5.m2_ref.refs_10_
  196.7 193.3 %wo_reduce.1 = (bf16[256,7168]{1,0:T(8,128)(2,1)}, f32[8,7168]{1,0:T(8,128)}, bf16[2,3,3,896,512]{4,3,2,1,0:T(8,128)(2,1)}, bf16[3,4,3,896,512]{4,3,2,1,0:T(8,128)(2,1)}) custom-call(bf16[512,4096]{1,0:T(8,128)(2,1)} %get-tuple-element.26.p_ref, bf16[16,4096]{1,0:T(8,128)(2,1)} %concatenate.49.q_ref, bf16[256,7168]{1,0:T(8,128)(2,1)} %dynamic-slice_bitcast_fusion.x_ref, ...), custom_call_target="tpu_custom_call" | custom-call | flops 31004295168 | bytes 58720256 | tf_op jit(solution)/shard_map/wo_reduce/pallas_call | solution.py:403
  390.1 128.9 %mlp_spread.1 = (bf16[512,7168]{1,0:T(8,128)(2,1)}, f32[8,7168]{1,0:T(8,128)}, bf16[3,896,512]{2,1,0:T(8,128)(2,1)}) custom-call(bf16[256,7168]{1,0:T(8,128)(2,1)} %get-tuple-element.33.refs_0_, f32[8,7168]{1,0:T(8,128)} %get-tuple-element.34.refs_1_, f32[1,7168]{1,0:T(1,128)} %convert_element_type.66.refs_2_, bf16[7168,512]{1,0:T(8,128)(2,1)} %bitcast.75, ...), custom_call_target="tpu_custom_call" | custom-call | flops 23957864448 | bytes 88080384 | tf_op jit(solution)/shard_map/mlp_spread/pallas_call | solution.py:670
  519.0 1.6 fusion.33
  520.6 6.6 %copy.127 = bf16[1,512,7168]{2,1,0:T(8,128)(2,1)} copy(bf16[1,512,7168]{2,1,0:T(8,128)(2,1)} %bitcast.76) | data formatting | bytes 14680064
  (39 shorter events, 0.3 us)
Async XLA Ops:
  2.4 5.0 copy-start.7
  2.5 5.1 copy-start.6
  2.5 5.1 copy-start
  6.1 64.4 %collective-permute-start = (bf16[3,896,512]{2,1,0:T(8,128)(2,1)}, bf16[3,896,512]{2,1,0:T(8,128)(2,1)}, u32[]{:S(2)}, u32[]{:S(2)}) collective-permute-start(bf16[3,896,512]{2,1,0:T(8,128)(2,1)} %pad_maximum_fusion), channel_id=1, source_target_pairs={{4,0},{8,12},{5,1},{9,13},{6,2},{10,14},{7,3},{11,15},{20,16},{24,... | collective-permute-start | bytes 8257544 | tf_op jit(solution)/shard_map/ppermute | solution.py:710
  7.6 20.7 %copy-start.9 = (s32[1,4]{1,0:T(1,128)S(1)}, s32[1,4]{1,0:T(1,128)}, u32[]{:S(2)}) copy-start(s32[1,4]{1,0:T(1,128)} %param.21) | copy-start | bytes 52
  24.8 3.0 copy-start.1
  29.8 28.5 %collective-permute-start.1 = (bf16[512,576]{0,1:T(8,128)(2,1)S(1)}, bf16[512,576]{0,1:T(8,128)(2,1)S(1)}, u32[]{:S(2)}, u32[]{:S(2)}) collective-permute-start(bf16[512,576]{0,1:T(8,128)(2,1)S(1)} %copy.83), channel_id=1, source_target_pairs={{0,1},{1,2},{2,3},{3,0},{4,5},{5,6},{6,7},{7,4},{8,9},{9,10},{10,1... | collective-permute-start | bytes 1769480 | tf_op jit(solution)/shard_map/ppermute | solution.py:753
  39.1 5.0 copy-start.11
  44.1 4.7 copy-start.10
  44.1 7.5 %copy-start.8 = (bf16[1,7168]{1,0:T(2,128)(2,1)S(1)}, bf16[1,7168]{1,0:T(2,128)(2,1)}, u32[]{:S(2)}) copy-start(bf16[1,7168]{1,0:T(2,128)(2,1)} %param.28) | copy-start | bytes 43012
  52.2 6.1 %copy-start.2 = (bf16[512,32,128]{0,2,1:T(8,128)(2,1)S(1)}, bf16[512,32,128]{0,2,1:T(8,128)(2,1)}, u32[]{:S(2)}) copy-start(bf16[512,32,128]{0,2,1:T(8,128)(2,1)} %copy.93) | copy-start | bytes 12582916
  70.5 126.2 %collective-permute-start.2 = (bf16[3,896,512]{2,1,0:T(8,128)(2,1)}, bf16[3,896,512]{2,1,0:T(8,128)(2,1)}, u32[]{:S(2)}, u32[]{:S(2)}) collective-permute-start(bf16[3,896,512]{2,1,0:T(8,128)(2,1)} %collective-permute-done.f0_ref.refs_6_), channel_id=1, source_target_pairs={{0,2},{1,3},{2,0},{3,1},{4,6},{5,7},{6,4},{7,5},{8,10},{9,11},{10,... | collective-permute-start | bytes 8257544 | tf_op jit(solution)/shard_map/ppermute | solution.py:714
  72.8 123.9 %collective-permute-start.3 = (bf16[3,896,512]{2,1,0:T(8,128)(2,1)}, bf16[3,896,512]{2,1,0:T(8,128)(2,1)}, u32[]{:S(2)}, u32[]{:S(2)}) collective-permute-start(bf16[3,896,512]{2,1,0:T(8,128)(2,1)} %collective-permute-done.f0_ref.refs_6_), channel_id=1, source_target_pairs={{0,16},{16,0},{1,17},{17,1},{2,18},{18,2},{3,19},{19,3},{4,20},{20... | collective-permute-start | bytes 8257544 | tf_op jit(solution)/shard_map/ppermute | solution.py:715
  74.3 122.4 %collective-permute-start.4 = (bf16[3,896,512]{2,1,0:T(8,128)(2,1)}, bf16[3,896,512]{2,1,0:T(8,128)(2,1)}, u32[]{:S(2)}, u32[]{:S(2)}) collective-permute-start(bf16[3,896,512]{2,1,0:T(8,128)(2,1)} %collective-permute-done.f0_ref.refs_6_), channel_id=1, source_target_pairs={{0,18},{1,19},{2,16},{3,17},{16,2},{17,3},{18,0},{19,1},{4,22},{5,... | collective-permute-start | bytes 8257544 | tf_op jit(solution)/shard_map/ppermute | solution.py:716
  74.3 122.4 %collective-permute-start.5 = (bf16[3,896,512]{2,1,0:T(8,128)(2,1)}, bf16[3,896,512]{2,1,0:T(8,128)(2,1)}, u32[]{:S(2)}, u32[]{:S(2)}) collective-permute-start(bf16[3,896,512]{2,1,0:T(8,128)(2,1)} %pad_maximum_fusion), channel_id=1, source_target_pairs={{8,0},{4,12},{9,1},{5,13},{10,2},{6,14},{11,3},{7,15},{24,16},{20,... | collective-permute-start | bytes 8257544 | tf_op jit(solution)/shard_map/ppermute | solution.py:710
  75.6 121.2 %collective-permute-start.6 = (bf16[3,896,512]{2,1,0:T(8,128)(2,1)}, bf16[3,896,512]{2,1,0:T(8,128)(2,1)}, u32[]{:S(2)}, u32[]{:S(2)}) collective-permute-start(bf16[3,896,512]{2,1,0:T(8,128)(2,1)} %pad_maximum_fusion), channel_id=1, source_target_pairs={{12,0},{0,12},{13,1},{1,13},{14,2},{2,14},{15,3},{3,15},{28,16},{1... | collective-permute-start | bytes 8257544 | tf_op jit(solution)/shard_map/ppermute | solution.py:710
  81.8 92.6 %copy-start.3 = (bf16[1,1,4,64,32,192]{5,4,3,2,1,0:T(8,128)(2,1)S(1)}, bf16[1,1,4,64,32,192]{5,4,3,2,1,0:T(8,128)(2,1)}, u32[]{:S(2)}) copy-start(bf16[1,1,4,64,32,192]{5,4,3,2,1,0:T(8,128)(2,1)} %param.19) | copy-start | bytes 9437188
  174.9 4.6 copy-start.5
  191.5 2.9 copy-start.4
